TPU v7x, 32 devices: a whole 2x2x4 slice. The times are simulated.
32 devices in a mesh: cuts: 4 (over z), tile: 8 (over y, x, core).
Axes of the slice: x: 2, y: 2, z: 4, core: 2. Of those that a mesh axis runs over, the one named last changes fastest.
Arguments:
- probe_wave: float32 [2, 256, 256], replicated, may hold values from -6 to 6
- transmission: float32 [4, 2, 4096, 2048], P('cuts', None, None, 'tile'), may hold values from -1 to 1, as said below
- kernel_phase: float32 [256, 256], replicated, may hold values from -3.140625 to 3.140625
- measured: bfloat16 [8, 6, 256, 256], P('tile'), may hold values from 0 to 4
- counts: int32 [8], P('tile'), may hold values from 1 to 6, as said below
- positions: int32 [8, 6, 2], P('tile'), may hold values from 0 to 3840, as said below
- widths: int32 [8, 2], P('tile'), may hold values from 32 to 128
Outputs:
- adjoint_wave: float32 [4, 8, 6, 2, 256, 256], P('cuts', 'tile')
- object_grad: float32 [4, 2, 4096, 2048], P('cuts', None, None, 'tile')
Inputs may be any that keep to these rules, and one draw needn't show every extreme that they name: Every entry has magnitude at most 1; each pair is a complex transmission. Tile t uses its first counts[t] slots; some tile uses all 6 slots. `positions`: rows lie in 0 to 3840 and columns in 0 to 256; column 0 of a tile's extended patch is 128 columns left of its first own column.
All inputs are finite; a program needn't handle non-finite values.
Results may differ from a plain program's by a relative error of at most 0.0003.
Values sent between devices are 32-bit elements; how exact they have to be, the bound alone decides.
A program may use at most 256 MiB of HBM per device.

v0:
```python
import functools
import math

import jax
import jax.numpy as jnp
import numpy as np
from jax import lax
from jax.experimental import pallas as pl
from jax.experimental.pallas import tpu as pltpu
from jax.sharding import PartitionSpec as P

RIM = 128
PAD = 8
MESH = pl.DeviceIdType.MESH
VMEM_LIMIT = 60 * 1024 * 1024


def params(**kw):
    return pltpu.CompilerParams(vmem_limit_bytes=VMEM_LIMIT, **kw)


def vmem():
    return pl.BlockSpec(memory_space=pltpu.VMEM)


def smem():
    return pl.BlockSpec(memory_space=pltpu.SMEM)


def shift(value, axis, by):
    count = lax.axis_size(axis)
    pairs = [(i, i + by) for i in range(count) if 0 <= i + by < count]
    return lax.ppermute(value, axis, pairs)


def make_tables(extent):
    half = extent // 2
    indices = np.arange(extent)
    angles = (indices[:, None] * indices[None, :] % extent) * (2.0 * math.pi / extent)
    cosine = (np.cos(angles) / math.sqrt(extent)).astype(np.float32)
    sine = (np.sin(angles) / math.sqrt(extent)).astype(np.float32)
    tables = []
    for parity in range(2):
        c, s = cosine[parity::2, :half], sine[parity::2, :half]
        block = np.block([[c, s], [-s, c]])
        for matrix in (block, block.T):
            hi = matrix.astype(jnp.bfloat16)
            lo = (matrix - hi.astype(np.float32)).astype(jnp.bfloat16)
            tables += [jnp.asarray(hi), jnp.asarray(lo)]
    order = np.concatenate([indices[0::2], indices[1::2]])
    sort = (order[:, None] == indices[None, :]).astype(jnp.bfloat16)
    return tables + [jnp.asarray(sort), jnp.asarray(np.ascontiguousarray(sort.T))]


def aligned(row, limit):
    base = jnp.minimum(row // PAD * PAD, limit)
    return pl.multiple_of(base, PAD), row - base


def extract_kernel(here, left_pos, right_pos, own_pos, trans, own, to_left, to_right,
                   buf_own, buf_left, buf_right, sems):
    slots, _, extent, _ = own.shape
    rows, cols = trans.shape[1:]
    tall = extent + PAD
    slack = cols + 2 * RIM - extent
    jobs = (
        (left_pos, buf_left, 0, RIM),
        (right_pos, buf_right, cols - RIM, RIM),
        (own_pos, buf_own, 0, cols),
    )

    def copy(j, s):
        pos, buf, start, width = jobs[j]
        base, off = aligned(pos[s, 0], rows - tall)
        src = trans.at[:, pl.ds(base, tall), pl.ds(start, width)]
        return pltpu.make_async_copy(src, buf.at[s], sems.at[j, s]), off

    for j in range(3):
        for s in range(slots):
            copy(j, s)[0].start()

    def columns(width):
        return lax.broadcasted_iota(jnp.int32, (extent, width), 1)

    def load(j, s, p, off, turn):
        value = pltpu.roll(jobs[j][1][s, p], (tall - off) % tall, 0)[:extent]
        return pltpu.roll(value, turn, 1)

    def for_left(s, carry):
        one, off = copy(0, s)
        one.wait()
        short = slack - left_pos[s, 1]
        at = columns(RIM) - short
        good = (at >= 0) & (at + 1 <= left_pos[slots, 1])
        for p in range(2):
            value = load(0, s, p, off, short % RIM)
            to_left[s, p] = jnp.where(good, value, 0.0)
        return carry

    def for_right(s, carry):
        one, off = copy(1, s)
        one.wait()
        col = right_pos[s, 1]
        at = columns(RIM) + col
        good = (at < RIM) & (RIM - at <= right_pos[slots, 0])
        for p in range(2):
            value = load(1, s, p, off, (cols - col) % RIM)
            to_right[s, p] = jnp.where(good, value, 0.0)
        return carry

    def for_own(s, carry):
        one, off = copy(2, s)
        one.wait()
        col = own_pos[s, 1]
        at = columns(extent) + col
        middle = (at >= RIM) & (at < RIM + cols)
        left_ok = (here[0] > 0) & (at < RIM) & (RIM - at <= own_pos[slots, 0])
        right_ok = (here[0] < here[1] - 1) & (at >= RIM + cols) & (
            at - RIM - cols + 1 <= own_pos[slots, 1])
        rim = left_ok | right_ok
        for p in range(2):
            value = load(2, s, p, off, (cols + RIM - col) % cols)
            out = jnp.where(rim, 0.0, 1.0 - p)
            own[s, p] = jnp.where(middle, value, out)
        return carry

    lax.fori_loop(0, slots, for_left, 0)
    lax.fori_loop(0, slots, for_right, 0)
    lax.fori_loop(0, slots, for_own, 0)


def gather_kernel(left_pos, right_pos, own_pos, contrib, from_left, from_right, out):
    slots, _, extent, _ = contrib.shape
    rows, cols = out.shape[1:]
    tall = extent + PAD
    slack = cols + 2 * RIM - extent
    out[...] = jnp.zeros(out.shape, out.dtype)

    def columns(width):
        return lax.broadcasted_iota(jnp.int32, (extent, width), 1)

    def add(source, s, pos, good, turn, start, width):
        base, off = aligned(pos[s, 0], rows - tall)
        for p in range(2):
            value = jnp.where(good, pltpu.roll(source[s, p], turn, 1), 0.0)
            value = jnp.concatenate([value, jnp.zeros((PAD, width), jnp.float32)], axis=0)
            value = pltpu.roll(value, off, 0)
            out[p, pl.ds(base, tall), pl.ds(start, width)] += value

    def body(s, carry):
        col = own_pos[s, 1]
        at = columns(cols) + RIM - col
        good = (at >= 0) & (at < extent)
        add(contrib, s, own_pos, good, (col + cols - RIM) % cols, 0, cols)
        short = slack - left_pos[s, 1]
        at = columns(RIM)
        good = (at + short < RIM) & (at + 1 <= left_pos[slots, 1])
        add(from_left, s, left_pos, good, (cols - short) % RIM, 0, RIM)
        col = right_pos[s, 1]
        good = (at >= col) & (RIM - at <= right_pos[slots, 0])
        add(from_right, s, right_pos, good, col % RIM, cols - RIM, RIM)
        return carry

    lax.fori_loop(0, slots, body, 0)


def pipeline_kernel(sections, tiles, live, to_left, to_right, own, probe, phase_kernel, measured,
                    ef_hi, ef_lo, ei_hi, ei_lo, of_hi, of_lo, oi_hi, oi_lo, sort, unsort, adjoint, contrib, from_left, from_right,
                    windows, left_rim, right_rim, got_left, got_right,
                    arrived, leaving, backed, lefts, rights, turn,
                    talls, wides, freq, spectrum, send_f, recv_f, send_b, recv_b,
                    send_rim, recv_rim, send_got, recv_got):
    g = lax.axis_index("cuts")
    t = lax.axis_index("tile")
    last = sections - 1
    end = tiles - 1
    slots, _, extent, _ = own.shape
    h = extent // 2

    barrier = pltpu.get_barrier_semaphore()

    @pl.when(g > 0)
    def _():
        pl.semaphore_signal(barrier, inc=1, device_id={"cuts": g - 1}, device_id_type=MESH)

    @pl.when(g < last)
    def _():
        pl.semaphore_signal(barrier, inc=1, device_id={"cuts": g + 1}, device_id_type=MESH)

    @pl.when(t > 0)
    def _():
        pl.semaphore_signal(barrier, inc=1, device_id={"tile": t - 1}, device_id_type=MESH)

    @pl.when(t < end)
    def _():
        pl.semaphore_signal(barrier, inc=1, device_id={"tile": t + 1}, device_id_type=MESH)

    peers = (g + last - 1) // last + 1 - g // last + (t + end - 1) // end + 1 - t // end
    pl.semaphore_wait(barrier, peers)

    def rim_copy(side, s):
        src, dst = ((to_left, right_rim), (to_right, left_rim))[side]
        return pltpu.make_async_remote_copy(
            src_ref=src.at[s], dst_ref=dst.at[s], send_sem=send_rim.at[side, s],
            recv_sem=recv_rim.at[side, s], device_id={"tile": t + (-1, 1)[side]},
            device_id_type=MESH)

    def got_copy(side, s):
        start, dst = ((0, got_right), (extent - RIM, got_left))[side]
        return pltpu.make_async_remote_copy(
            src_ref=contrib.at[s, :, :, pl.ds(start, RIM)], dst_ref=dst.at[s],
            send_sem=send_got.at[side, s], recv_sem=recv_got.at[side, s],
            device_id={"tile": t + (-1, 1)[side]}, device_id_type=MESH)

    def each(action):
        def body(s, carry):
            action(s)
            return carry

        lax.fori_loop(0, slots, body, 0)

    @pl.when(t > 0)
    def _():
        each(lambda s: rim_copy(0, s).start())

    @pl.when(t < end)
    def _():
        each(lambda s: rim_copy(1, s).start())

    @pl.when(t == 0)
    def _():
        left_rim[...] = jnp.zeros(left_rim.shape, left_rim.dtype)
        got_left[...] = jnp.zeros(got_left.shape, got_left.dtype)

    @pl.when(t == end)
    def _():
        right_rim[...] = jnp.zeros(right_rim.shape, right_rim.dtype)
        got_right[...] = jnp.zeros(got_right.shape, got_right.dtype)

    forms = ((ef_hi, ef_lo, ei_hi, ei_lo), (of_hi, of_lo, oi_hi, oi_lo))
    for parity in range(2):
        fh, fl, ih, il = forms[parity]
        for inverse, (lh, ll, rh, rl) in enumerate(((fh, fl, ih, il), (ih, il, fh, fl))):
            at = 2 * inverse + parity
            lefts[at, :, :extent] = lh[...]
            lefts[at, :, extent : 2 * extent] = lh[...]
            lefts[at, :, 2 * extent :] = ll[...]
            rights[at, :extent] = rh[...]
            rights[at, extent : 2 * extent] = rh[...]
            rights[at, 2 * extent :] = rl[...]

    def exact(x, y):
        return jnp.dot(x, y, preferred_element_type=jnp.float32)

    for p in range(2):
        rest = phase_kernel[p]
        total = jnp.zeros((extent, extent), jnp.float32)
        for _ in range(3):
            part = rest.astype(jnp.bfloat16)
            rest = rest - part.astype(jnp.float32)
            rows = exact(sort[...], part).astype(jnp.bfloat16)
            total += exact(rows, unsort[...])
        turn[p] = total

    def split(value):
        hi = value.astype(jnp.bfloat16)
        lo = (value - hi.astype(jnp.float32)).astype(jnp.bfloat16)
        return (hi, lo, hi)

    def put_tall(parity, p, value):
        for at, part in enumerate(split(value)):
            talls[parity, pl.ds(at * extent + p * h, h), :] = part

    def put_wide(parity, rows, p, value):
        n = value.shape[0]
        for at, part in enumerate(split(value)):
            wides[parity, pl.ds(rows, n), pl.ds(at * extent + p * h, h)] = part

    def left(at):
        return exact(lefts[at], talls[at % 2])

    def right(at):
        return exact(wides[at % 2], rights[at])

    def to_freq(pair):
        for p in range(2):
            put_tall(0, p, pair[p][:h] + pair[p][h:])
            put_tall(1, p, pair[p][:h] - pair[p][h:])
        for block in range(2):
            half = left(block)
            for p in range(2):
                value = half[p * h : (p + 1) * h]
                put_wide(0, block * h, p, value[:, :h] + value[:, h:])
                put_wide(1, block * h, p, value[:, :h] - value[:, h:])
        for parity in range(2):
            freq[parity] = right(parity)

    def from_freq():
        u, v = right(2), right(3)
        for p in range(2):
            up, vp = u[:, p * h : (p + 1) * h], v[:, p * h : (p + 1) * h]
            plus, minus = up + vp, up - vp
            for parity in range(2):
                rows = slice(parity * h, (parity + 1) * h)
                both = jnp.concatenate([plus[rows], minus[rows]], axis=1)
                put_tall(parity, p, both)
        u, v = left(2), left(3)
        for p in range(2):
            up, vp = u[p * h : (p + 1) * h], v[p * h : (p + 1) * h]
            spectrum[p, :h] = up + vp
            spectrum[p, h:] = up - vp

    def propagate(pair, sign):
        to_freq(pair)
        for parity in range(2):
            cols = slice(parity * h, (parity + 1) * h)
            kr, ki = turn[0, :, cols], sign * turn[1, :, cols]
            xr, xi = freq[parity, :, :h], freq[parity, :, h:]
            put_wide(parity, 0, 0, kr * xr - ki * xi)
            put_wide(parity, 0, 1, kr * xi + ki * xr)
        from_freq()

    def send_forward(s):
        return pltpu.make_async_remote_copy(
            src_ref=leaving.at[s], dst_ref=arrived.at[s], send_sem=send_f.at[s],
            recv_sem=recv_f.at[s], device_id={"cuts": g + 1}, device_id_type=MESH)

    def send_backward(s):
        return pltpu.make_async_remote_copy(
            src_ref=adjoint.at[s], dst_ref=backed.at[s], send_sem=send_b.at[s],
            recv_sem=recv_b.at[s], device_id={"cuts": g - 1}, device_id_type=MESH)

    def forward(s):
        @pl.when(g == 0)
        def _():
            arrived[s] = probe[...] * live[s]

        @pl.when(g > 0)
        def _():
            send_forward(s).wait_recv()

        @pl.when(t < end)
        def _():
            rim_copy(0, s).wait_recv()

        @pl.when(t > 0)
        def _():
            rim_copy(1, s).wait_recv()

        for p in range(2):
            windows[s, p, :, :RIM] = own[s, p, :, :RIM] + left_rim[s, p]
            if extent > 2 * RIM:
                windows[s, p, :, RIM : extent - RIM] = own[s, p, :, RIM : extent - RIM]
            windows[s, p, :, extent - RIM :] = own[s, p, :, extent - RIM :] + right_rim[s, p]
        wr, wi = windows[s, 0], windows[s, 1]
        xr, xi = arrived[s, 0], arrived[s, 1]
        propagate((wr * xr - wi * xi, wr * xi + wi * xr), 1.0)

        @pl.when(g < last)
        def _():
            leaving[s, 0] = spectrum[0]
            leaving[s, 1] = spectrum[1]
            send_forward(s).start()

    def backward(s):
        @pl.when(g == last)
        def _():
            seen = exact(sort[...], measured[s]).astype(jnp.bfloat16)
            seen = exact(seen, unsort[...])
            to_freq((spectrum[0], spectrum[1]))
            for parity in range(2):
                fr, fi = freq[parity, :, :h], freq[parity, :, h:]
                residual = fr * fr + fi * fi - seen[:, parity * h : (parity + 1) * h]
                put_wide(parity, 0, 0, fr * residual)
                put_wide(parity, 0, 1, fi * residual)
            from_freq()

        @pl.when(g < last)
        def _():
            send_backward(s).wait_recv()
            spectrum[0] = backed[s, 0]
            spectrum[1] = backed[s, 1]

        propagate((spectrum[0], spectrum[1]), -1.0)
        tr, ti = spectrum[0], spectrum[1]
        wr, wi = windows[s, 0], windows[s, 1]
        br, bi = wr * tr + wi * ti, wr * ti - wi * tr

        adjoint[s, 0] = br
        adjoint[s, 1] = bi

        @pl.when(g > 0)
        def _():
            send_backward(s).start()

        xr, xi = arrived[s, 0], arrived[s, 1]
        contrib[s, 0] = xr * tr + xi * ti
        contrib[s, 1] = xr * ti - xi * tr

        @pl.when(t > 0)
        def _():
            got_copy(0, s).start()

        @pl.when(t < end)
        def _():
            got_copy(1, s).start()

    lag = 2 * (last - g)

    def step(k, carry):
        @pl.when(k < slots)
        def _():
            forward(k)

        @pl.when((k >= lag) & (k < lag + slots))
        def _():
            backward(k - lag)

        return carry

    lax.fori_loop(0, slots + 2 * last, step, 0)

    @pl.when(g < last)
    def _():
        each(lambda s: send_forward(s).wait_send())

    @pl.when(g > 0)
    def _():
        each(lambda s: send_backward(s).wait_send())

    @pl.when(t < end)
    def _():
        each(lambda s: got_copy(0, s).wait_recv())

    @pl.when(t > 0)
    def _():
        each(lambda s: got_copy(1, s).wait_recv())

    def finish(side):
        def body(s):
            rim_copy(side, s).wait_send()
            got_copy(side, s).wait_send()

        each(body)

    @pl.when(t > 0)
    def _():
        finish(0)

    @pl.when(t < end)
    def _():
        finish(1)

    from_left[...] = got_left[...]
    from_right[...] = got_right[...]


def on_device(probe_wave, transmission, kernel_phase, measured, counts, positions, widths):
    f32 = jnp.float32
    rows, cols = transmission.shape[2:]
    extent = probe_wave.shape[-1]
    slots = positions.shape[1]
    sections = lax.axis_size("cuts")
    tiles_total = lax.axis_size("tile")
    tile_at = lax.axis_index("tile")
    tall = extent + PAD
    trans = transmission[0]
    own_pos = jnp.concatenate([positions[0], widths], 0)
    right_pos = shift(own_pos, "tile", -1)
    left_pos = shift(own_pos, "tile", 1)
    here = jnp.stack([tile_at, jnp.asarray(tiles_total, tile_at.dtype)]).astype(jnp.int32)
    sds = jax.ShapeDtypeStruct
    wave = sds((slots, 2, extent, extent), f32)
    rim = sds((slots, 2, extent, RIM), f32)
    assert extent == cols and extent >= 2 * RIM

    own, to_left, to_right = pl.pallas_call(
        extract_kernel,
        out_shape=(wave, rim, rim),
        in_specs=[smem()] * 4 + [pl.BlockSpec(memory_space=pl.ANY)],
        out_specs=(vmem(), vmem(), vmem()),
        scratch_shapes=[
            pltpu.VMEM((slots, 2, tall, cols), f32),
            pltpu.VMEM((slots, 2, tall, RIM), f32),
            pltpu.VMEM((slots, 2, tall, RIM), f32),
            pltpu.SemaphoreType.DMA((3, slots)),
        ],
        compiler_params=params(),
    )(here, left_pos, right_pos, own_pos, trans)

    tables = make_tables(extent)
    phase_kernel = jnp.stack([jnp.cos(kernel_phase), jnp.sin(kernel_phase)], 0)
    live = (jnp.arange(slots, dtype=jnp.int32) < counts[0]).astype(f32)
    waves = pltpu.VMEM((slots, 2, extent, extent), f32)
    bf16 = jnp.bfloat16
    rims = pltpu.VMEM((slots, 2, extent, RIM), f32)
    adjoint, contrib, from_left, from_right = pl.pallas_call(
        functools.partial(pipeline_kernel, sections, tiles_total),
        out_shape=(wave, wave, rim, rim),
        in_specs=[smem()] + [vmem()] * 16,
        out_specs=(vmem(),) * 4,
        scratch_shapes=[
            waves, rims, rims, rims, rims,
            waves, waves, waves,
            pltpu.VMEM((4, extent, 3 * extent), bf16),
            pltpu.VMEM((4, 3 * extent, extent), bf16),
            pltpu.VMEM((2, extent, extent), f32),
            pltpu.VMEM((2, 3 * extent, extent), bf16),
            pltpu.VMEM((2, extent, 3 * extent), bf16),
            pltpu.VMEM((2, extent, extent), f32),
            pltpu.VMEM((2, extent, extent), f32),
            pltpu.SemaphoreType.DMA((slots,)),
            pltpu.SemaphoreType.DMA((slots,)),
            pltpu.SemaphoreType.DMA((slots,)),
            pltpu.SemaphoreType.DMA((slots,)),
            pltpu.SemaphoreType.DMA((2, slots)),
            pltpu.SemaphoreType.DMA((2, slots)),
            pltpu.SemaphoreType.DMA((2, slots)),
            pltpu.SemaphoreType.DMA((2, slots)),
        ],
        compiler_params=params(collective_id=0, has_side_effects=True),
    )(live, to_left, to_right, own, probe_wave, phase_kernel, measured[0], *tables)

    grad = pl.pallas_call(
        gather_kernel,
        out_shape=sds((2, rows, cols), f32),
        in_specs=[smem()] * 3 + [vmem()] * 3,
        out_specs=vmem(),
        compiler_params=params(),
    )(left_pos, right_pos, own_pos, contrib, from_left, from_right)
    return (adjoint[None, None], grad[None])


def solution(mesh):
    return jax.shard_map(
        on_device,
        mesh=mesh,
        in_specs=(
            P(),
            P("cuts", None, None, "tile"),
            P(),
            P("tile", None, None, None),
            P("tile"),
            P("tile", None, None),
            P("tile", None),
        ),
        out_specs=(P("cuts", "tile", None, None, None, None), P("cuts", None, None, "tile")),
        check_vma=False,
    )
```

profile of v0, /device:TPU:3, one launch (start us, length us, event | category | flops | bytes accessed | tf_op | source)
XLA Modules:
  0.0 201.6 jit_solution(18379106596921026202)
XLA Ops:
  0.6 0.8 copy.25
  1.4 0.7 pad_add_fusion.own_pos
  2.1 0.0 copy-start.1
  2.1 2.6 %collective-permute-start.1 = (s32[7,2]{1,0:T(8,128)S(1)}, s32[7,2]{1,0:T(8,128)S(1)}, u32[]{:S(2)}, u32[]{:S(2)}) collective-permute-start(s32[7,2]{1,0:T(8,128)S(1)} %pad_add_fusion.own_pos), channel_id=1, source_target_pairs={{1,0},{2,1},{3,2},{4,3},{5,4},{6,5},{7,6},{9,8},{10,9},{11,10},{12... | collective-permute-start | bytes 176 | tf_op jit(solution)/shard_map/ppermute | solution.py:33
  4.6 3.9 %collective-permute-start = (s32[7,2]{1,0:T(8,128)S(1)}, s32[7,2]{1,0:T(8,128)S(1)}, u32[]{:S(2)}, u32[]{:S(2)}) collective-permute-start(s32[7,2]{1,0:T(8,128)S(1)} %pad_add_fusion.own_pos), channel_id=1, source_target_pairs={{0,1},{1,2},{2,3},{3,4},{4,5},{5,6},{6,7},{8,9},{9,10},{10,11},{11... | collective-permute-start | bytes 176 | tf_op jit(solution)/shard_map/ppermute | solution.py:33
  9.2 0.6 compare_convert_fusion.live
  9.8 1.9 cosine_bitcast_fusion
  11.6 0.8 pad_maximum_fusion.phase_kernel
  12.5 0.7 pad_add_fusion.1.here
  13.1 0.0 collective-permute-done.1.right_pos
  13.1 0.0 copy-start.2
  13.1 0.0 collective-permute-done.left_pos
  13.1 0.0 copy-start.3
  13.1 0.0 copy-done.1
  13.1 0.6 copy-done.2
  13.7 0.0 copy-done.3
  13.7 8.7 %shard_map.176 = (f32[6,2,256,256]{3,2,1,0:T(8,128)}, f32[6,2,256,128]{3,2,1,0:T(8,128)}, f32[6,2,256,128]{3,2,1,0:T(8,128)}) custom-call(s32[2]{0:T(128)} %pad_add_fusion.1.here, s32[7,2]{1,0:T(8,128)} %copy-done.3, s32[7,2]{1,0:T(8,128)} %copy-done.2, s32[7,2]{1,0:T(8,128)} %copy-done.1, f32[2,4096,256]{2,1,0:T(8,128)} %bitcast.12), custom_call_target="tpu_custom_call" | custom-call | tf_op jit(solution)/shard_map/pallas_call | solution.py:477
  22.4 167.2 %shard_map.177 = (f32[6,2,256,256]{3,2,1,0:T(8,128)}, f32[6,2,256,256]{3,2,1,0:T(8,128)}, f32[6,2,256,128]{3,2,1,0:T(8,128)}, f32[6,2,256,128]{3,2,1,0:T(8,128)}) custom-call(f32[6]{0:T(128)} %compare_convert_fusion.live, f32[6,2,256,128]{3,2,1,0:T(8,128)} %get-tuple-element.9.to_left, f32[6,2,256,128]{3,2,1,0:T(8,128)} %get-tuple-element.10.to_right, ...), custom_call_target="tpu_custom_call" | custom-call | tf_op jit(solution)/shard_map/pallas_call | solution.py:497
  189.6 0.0 copy-start
  189.6 10.4 %shard_map.178 = f32[2,4096,256]{2,1,0:T(8,128)} custom-call(s32[7,2]{1,0:T(8,128)} %copy-done.3, s32[7,2]{1,0:T(8,128)} %copy-done.2, s32[7,2]{1,0:T(8,128)} %copy-done.1, f32[6,2,256,256]{3,2,1,0:T(8,128)} %get-tuple-element.13.contrib, f32[6,2,256,128]{3,2,1,0:T(8,128)} %get-tuple-element.14.from_left, f32[6,2,256,128]{3,2,1,0:T(8,128)} %get-tuple-element.15.from_right), custom_call_target="tpu_custom_call" | custom-call | tf_op jit(solution)/shard_map/pallas_call | solution.py:524
  200.0 0.0 copy-done
  200.0 1.7 copy.28
Async XLA Ops:
  2.1 11.1 %copy-start.1 = (s32[7,2]{1,0:T(8,128)}, s32[7,2]{1,0:T(8,128)S(1)}, u32[]{:S(2)}) copy-start(s32[7,2]{1,0:T(8,128)S(1)} %pad_add_fusion.own_pos) | copy-start | bytes 172
  2.1 11.1 %collective-permute-start.1 = (s32[7,2]{1,0:T(8,128)S(1)}, s32[7,2]{1,0:T(8,128)S(1)}, u32[]{:S(2)}, u32[]{:S(2)}) collective-permute-start(s32[7,2]{1,0:T(8,128)S(1)} %pad_add_fusion.own_pos), channel_id=1, source_target_pairs={{1,0},{2,1},{3,2},{4,3},{5,4},{6,5},{7,6},{9,8},{10,9},{11,10},{12... | collective-permute-start | bytes 176 | tf_op jit(solution)/shard_map/ppermute | solution.py:33
  4.6 8.5 %collective-permute-start = (s32[7,2]{1,0:T(8,128)S(1)}, s32[7,2]{1,0:T(8,128)S(1)}, u32[]{:S(2)}, u32[]{:S(2)}) collective-permute-start(s32[7,2]{1,0:T(8,128)S(1)} %pad_add_fusion.own_pos), channel_id=1, source_target_pairs={{0,1},{1,2},{2,3},{3,4},{4,5},{5,6},{6,7},{8,9},{9,10},{10,11},{11... | collective-permute-start | bytes 176 | tf_op jit(solution)/shard_map/ppermute | solution.py:33
  13.1 0.6 copy-start.2
  13.1 0.6 copy-start.3
  189.6 10.4 %copy-start = (f32[6,2,256,256]{3,2,1,0:T(8,128)S(1)}, f32[6,2,256,256]{3,2,1,0:T(8,128)}, u32[]{:S(2)}) copy-start(f32[6,2,256,256]{3,2,1,0:T(8,128)} %get-tuple-element.12) | copy-start | bytes 9437188
where the time goes:
time: 202 us
  Pallas kernels  186 us (92%)
  starting transfers between devices  6.46 us (3%)
  local copies, waits for them, and re-layouts  4.86 us (2%)
  other arithmetic  2.73 us (1%)
    pallas_call x1, Pallas kernels, on_device(): pl.pallas_call(functools.partial(pipeline_kernel, sections, tiles_total),...  167 us
    pallas_call x1, Pallas kernels, on_device(): pl.pallas_call(gather_kernel, out_shape=sds((2, rows, cols), f32), in_spe...  10.4 us
    pallas_call x1, Pallas kernels, on_device(): pl.pallas_call(extract_kernel, out_shape=(wave, rim, rim), in_specs=[smem...  8.66 us
    ppermute x2, starting transfers between devices, shift(): return lax.ppermute(value, axis, pairs)  6.46 us
  transfers between devices with their start and end apart: 2, of which 0 were waited for; matrix products, arithmetic and copies ran while one was open for 2% of the time, Pallas kernels for 0%

commit v1 on v0

--- a/solution.py
+++ b/solution.py
@@ -167,15 +167,17 @@
 def pipeline_kernel(sections, tiles, live, to_left, to_right, own, probe, phase_kernel, measured,
                     ef_hi, ef_lo, ei_hi, ei_lo, of_hi, of_lo, oi_hi, oi_lo, sort, unsort, adjoint, contrib, from_left, from_right,
                     windows, left_rim, right_rim, got_left, got_right,
-                    arrived, leaving, backed, lefts, rights, turn,
+                    arrived, leaving, backed, ahead, lefts, rights, turn,
                     talls, wides, freq, spectrum, send_f, recv_f, send_b, recv_b,
-                    send_rim, recv_rim, send_got, recv_got):
+                    send_w, recv_w, send_rim, recv_rim, send_got, recv_got, token):
     g = lax.axis_index("cuts")
     t = lax.axis_index("tile")
     last = sections - 1
+    mid = last - 1
     end = tiles - 1
     slots, _, extent, _ = own.shape
     h = extent // 2
+    partner = t + 1 - 2 * (t % 2)
 
     barrier = pltpu.get_barrier_semaphore()
 
@@ -261,6 +263,7 @@
             rows = exact(sort[...], part).astype(jnp.bfloat16)
             total += exact(rows, unsort[...])
         turn[p] = total
+    turn[2] = -turn[1]
 
     def split(value):
         hi = value.astype(jnp.bfloat16)
@@ -282,10 +285,10 @@
     def right(at):
         return exact(wides[at % 2], rights[at])
 
-    def to_freq(pair):
-        for p in range(2):
-            put_tall(0, p, pair[p][:h] + pair[p][h:])
-            put_tall(1, p, pair[p][:h] - pair[p][h:])
+    def to_freq():
+        for p in range(2):
+            put_tall(0, p, spectrum[p, :h] + spectrum[p, h:])
+            put_tall(1, p, spectrum[p, :h] - spectrum[p, h:])
         for block in range(2):
             half = left(block)
             for p in range(2):
@@ -310,35 +313,22 @@
             spectrum[p, :h] = up + vp
             spectrum[p, h:] = up - vp
 
-    def propagate(pair, sign):
-        to_freq(pair)
-        for parity in range(2):
-            cols = slice(parity * h, (parity + 1) * h)
-            kr, ki = turn[0, :, cols], sign * turn[1, :, cols]
-            xr, xi = freq[parity, :, :h], freq[parity, :, h:]
-            put_wide(parity, 0, 0, kr * xr - ki * xi)
-            put_wide(parity, 0, 1, kr * xi + ki * xr)
-        from_freq()
-
-    def send_forward(s):
+    def send_forward(s, part):
         return pltpu.make_async_remote_copy(
-            src_ref=leaving.at[s], dst_ref=arrived.at[s], send_sem=send_f.at[s],
-            recv_sem=recv_f.at[s], device_id={"cuts": g + 1}, device_id_type=MESH)
+            src_ref=leaving.at[s, part], dst_ref=arrived.at[s, part], send_sem=send_f.at[s, part],
+            recv_sem=recv_f.at[s, part], device_id={"cuts": g + 1}, device_id_type=MESH)
 
     def send_backward(s):
         return pltpu.make_async_remote_copy(
             src_ref=adjoint.at[s], dst_ref=backed.at[s], send_sem=send_b.at[s],
             recv_sem=recv_b.at[s], device_id={"cuts": g - 1}, device_id_type=MESH)
 
-    def forward(s):
-        @pl.when(g == 0)
-        def _():
-            arrived[s] = probe[...] * live[s]
-
-        @pl.when(g > 0)
-        def _():
-            send_forward(s).wait_recv()
-
+    def send_window(s):
+        return pltpu.make_async_remote_copy(
+            src_ref=windows.at[s], dst_ref=ahead.at[s], send_sem=send_w.at[s],
+            recv_sem=recv_w.at[s], device_id={"cuts": g - 1}, device_id_type=MESH)
+
+    def compose(s):
         @pl.when(t < end)
         def _():
             rim_copy(0, s).wait_recv()
@@ -352,81 +342,150 @@
             if extent > 2 * RIM:
                 windows[s, p, :, RIM : extent - RIM] = own[s, p, :, RIM : extent - RIM]
             windows[s, p, :, extent - RIM :] = own[s, p, :, extent - RIM :] + right_rim[s, p]
-        wr, wi = windows[s, 0], windows[s, 1]
-        xr, xi = arrived[s, 0], arrived[s, 1]
-        propagate((wr * xr - wi * xi, wr * xi + wi * xr), 1.0)
-
-        @pl.when(g < last)
-        def _():
-            leaving[s, 0] = spectrum[0]
-            leaving[s, 1] = spectrum[1]
-            send_forward(s).start()
-
-    def backward(s):
-        @pl.when(g == last)
+
+    def product(w, x, s, sign):
+        wr, wi = w[s, 0], w[s, 1]
+        xr, xi = x
+        spectrum[0] = wr * xr - sign * (wi * xi)
+        spectrum[1] = wr * xi + sign * (wi * xr)
+
+    @pl.when(g == last)
+    def _():
+        def body(s):
+            compose(s)
+            send_window(s).start()
+
+        each(body)
+
+    def event(s, op):
+        @pl.when(op == 0)
+        def _():
+            @pl.when(g == 0)
+            def _():
+                arrived[s] = probe[...] * live[s]
+
+            @pl.when(g > 0)
+            def _():
+                send_forward(s, 0).wait_recv()
+                send_forward(s, 1).wait_recv()
+
+            @pl.when(g < last)
+            def _():
+                compose(s)
+
+            product(windows, (arrived[s, 0], arrived[s, 1]), s, 1.0)
+
+        @pl.when(op == 1)
+        def _():
+            send_window(s).wait_recv()
+            product(ahead, (spectrum[0], spectrum[1]), s, 1.0)
+
+        @pl.when((op == 4) & (g < mid))
+        def _():
+            send_backward(s).wait_recv()
+            spectrum[...] = backed[s]
+
+        @pl.when((op == 4) & (g == mid))
+        def _():
+            product(ahead, (spectrum[0], spectrum[1]), s, -1.0)
+
+        to_freq()
+
+        @pl.when(op == 2)
         def _():
             seen = exact(sort[...], measured[s]).astype(jnp.bfloat16)
             seen = exact(seen, unsort[...])
-            to_freq((spectrum[0], spectrum[1]))
             for parity in range(2):
                 fr, fi = freq[parity, :, :h], freq[parity, :, h:]
                 residual = fr * fr + fi * fi - seen[:, parity * h : (parity + 1) * h]
                 put_wide(parity, 0, 0, fr * residual)
                 put_wide(parity, 0, 1, fi * residual)
-            from_freq()
-
-        @pl.when(g < last)
-        def _():
-            send_backward(s).wait_recv()
-            spectrum[0] = backed[s, 0]
-            spectrum[1] = backed[s, 1]
-
-        propagate((spectrum[0], spectrum[1]), -1.0)
-        tr, ti = spectrum[0], spectrum[1]
-        wr, wi = windows[s, 0], windows[s, 1]
-        br, bi = wr * tr + wi * ti, wr * ti - wi * tr
-
-        adjoint[s, 0] = br
-        adjoint[s, 1] = bi
-
-        @pl.when(g > 0)
-        def _():
-            send_backward(s).start()
-
-        xr, xi = arrived[s, 0], arrived[s, 1]
-        contrib[s, 0] = xr * tr + xi * ti
-        contrib[s, 1] = xr * ti - xi * tr
-
-        @pl.when(t > 0)
-        def _():
-            got_copy(0, s).start()
-
-        @pl.when(t < end)
-        def _():
-            got_copy(1, s).start()
-
-    lag = 2 * (last - g)
-
-    def step(k, carry):
-        @pl.when(k < slots)
-        def _():
-            forward(k)
-
-        @pl.when((k >= lag) & (k < lag + slots))
-        def _():
-            backward(k - lag)
+
+        @pl.when(op != 2)
+        def _():
+            sine = 1 + op // 3
+            for parity in range(2):
+                cols = slice(parity * h, (parity + 1) * h)
+                kr, ki = turn[0, :, cols], turn[sine, :, cols]
+                xr, xi = freq[parity, :, :h], freq[parity, :, h:]
+                put_wide(parity, 0, 0, kr * xr - ki * xi)
+                put_wide(parity, 0, 1, kr * xi + ki * xr)
+
+        from_freq()
+
+        @pl.when((op == 0) & (g < last))
+        def _():
+            leaving[s] = spectrum[...]
+
+            @pl.when((g == 0) & ((s > 0) | (t % 2 == 1)))
+            def _():
+                pl.semaphore_wait(token, 1)
+
+            send_forward(s, 0).start()
+            send_forward(s, 1).start()
+
+            @pl.when(g == 0)
+            def _():
+                send_forward(s, 0).wait_send()
+
+                @pl.when((s < slots - 1) | (t % 2 == 0))
+                def _():
+                    pl.semaphore_signal(token, inc=1, device_id={"tile": partner}, device_id_type=MESH)
+
+        @pl.when(((op == 3) & (g == last)) | (op == 4))
+        def _():
+            tr, ti = spectrum[0], spectrum[1]
+            wr, wi = windows[s, 0], windows[s, 1]
+            adjoint[s, 0] = wr * tr + wi * ti
+            adjoint[s, 1] = wr * ti - wi * tr
+
+            @pl.when((g > 0) & (g < last))
+            def _():
+                send_backward(s).start()
+
+            xr, xi = arrived[s, 0], arrived[s, 1]
+            contrib[s, 0] = xr * tr + xi * ti
+            contrib[s, 1] = xr * ti - xi * tr
+
+            @pl.when(t > 0)
+            def _():
+                got_copy(0, s).start()
+
+            @pl.when(t < end)
+            def _():
+                got_copy(1, s).start()
+
+    lag = 2 * (mid - g)
+    early = (g < mid).astype(jnp.int32)
+    final = g // last
+    ops = 5 - 3 * early - 2 * final
+    count = (slots + early * lag) * ops
+
+    def step(e, carry):
+        k, part = e // ops, e % ops
+        s = k - early * part * lag
+        op = part + early * part * 3 + final * ((part + 1) // 2)
+
+        @pl.when((s >= 0) & (s < slots))
+        def _():
+            event(s, op)
 
         return carry
 
-    lax.fori_loop(0, slots + 2 * last, step, 0)
+    lax.fori_loop(0, count, step, 0)
 
     @pl.when(g < last)
     def _():
-        each(lambda s: send_forward(s).wait_send())
-
-    @pl.when(g > 0)
-    def _():
+        each(lambda s: send_forward(s, 1).wait_send())
+
+    @pl.when((g > 0) & (g < last))
+    def _():
+        each(lambda s: send_forward(s, 0).wait_send())
         each(lambda s: send_backward(s).wait_send())
+
+    @pl.when(g == last)
+    def _():
+        each(lambda s: send_window(s).wait_send())
 
     @pl.when(t < end)
     def _():
@@ -501,14 +560,16 @@
         out_specs=(vmem(),) * 4,
         scratch_shapes=[
             waves, rims, rims, rims, rims,
-            waves, waves, waves,
+            waves, waves, waves, waves,
             pltpu.VMEM((4, extent, 3 * extent), bf16),
             pltpu.VMEM((4, 3 * extent, extent), bf16),
-            pltpu.VMEM((2, extent, extent), f32),
+            pltpu.VMEM((3, extent, extent), f32),
             pltpu.VMEM((2, 3 * extent, extent), bf16),
             pltpu.VMEM((2, extent, 3 * extent), bf16),
             pltpu.VMEM((2, extent, extent), f32),
             pltpu.VMEM((2, extent, extent), f32),
+            pltpu.SemaphoreType.DMA((slots, 2)),
+            pltpu.SemaphoreType.DMA((slots, 2)),
             pltpu.SemaphoreType.DMA((slots,)),
             pltpu.SemaphoreType.DMA((slots,)),
             pltpu.SemaphoreType.DMA((slots,)),
@@ -517,6 +578,7 @@
             pltpu.SemaphoreType.DMA((2, slots)),
             pltpu.SemaphoreType.DMA((2, slots)),
             pltpu.SemaphoreType.DMA((2, slots)),
+            pltpu.SemaphoreType.REGULAR,
         ],
         compiler_params=params(collective_id=0, has_side_effects=True),
     )(live, to_left, to_right, own, probe_wave, phase_kernel, measured[0], *tables)

time: 202 us -> 176 us (0.87)
  Pallas kernels: 186 us -> 161 us
    pallas_call x1, Pallas kernels: 167 us -> 142 us  [on_device(): pl.pallas_call(functools.partial(pipeline_kernel, sections, tiles_total),...]
where the time goes in v1:
time: 176 us
  Pallas kernels  161 us (91%)
  starting transfers between devices  6.46 us (4%)
  local copies, waits for them, and re-layouts  4.86 us (3%)
  other arithmetic  2.73 us (2%)
    pallas_call x1, Pallas kernels, on_device(): pl.pallas_call(functools.partial(pipeline_kernel, sections, tiles_total),...  142 us
    pallas_call x1, Pallas kernels, on_device(): pl.pallas_call(gather_kernel, out_shape=sds((2, rows, cols), f32), in_spe...  10.3 us
    pallas_call x1, Pallas kernels, on_device(): pl.pallas_call(extract_kernel, out_shape=(wave, rim, rim), in_specs=[smem...  8.66 us
    ppermute x2, starting transfers between devices, shift(): return lax.ppermute(value, axis, pairs)  6.46 us
  transfers between devices with their start and end apart: 2, of which 0 were waited for; matrix products, arithmetic and copies ran while one was open for 2% of the time, Pallas kernels for 0%

profile of v1, /device:TPU:3, one launch (start us, length us, event | category | flops | bytes accessed | tf_op | source)
XLA Modules:
  0.0 175.9 jit_solution(17091154522901943009)
XLA Ops:
  0.6 0.8 copy.25
  1.4 0.7 pad_add_fusion.own_pos
  2.1 0.0 copy-start.1
  2.1 2.6 %collective-permute-start.1 = (s32[7,2]{1,0:T(8,128)S(1)}, s32[7,2]{1,0:T(8,128)S(1)}, u32[]{:S(2)}, u32[]{:S(2)}) collective-permute-start(s32[7,2]{1,0:T(8,128)S(1)} %pad_add_fusion.own_pos), channel_id=1, source_target_pairs={{1,0},{2,1},{3,2},{4,3},{5,4},{6,5},{7,6},{9,8},{10,9},{11,10},{12... | collective-permute-start | bytes 176 | tf_op jit(solution)/shard_map/ppermute | solution.py:33
  4.6 3.9 %collective-permute-start = (s32[7,2]{1,0:T(8,128)S(1)}, s32[7,2]{1,0:T(8,128)S(1)}, u32[]{:S(2)}, u32[]{:S(2)}) collective-permute-start(s32[7,2]{1,0:T(8,128)S(1)} %pad_add_fusion.own_pos), channel_id=1, source_target_pairs={{0,1},{1,2},{2,3},{3,4},{4,5},{5,6},{6,7},{8,9},{9,10},{10,11},{11... | collective-permute-start | bytes 176 | tf_op jit(solution)/shard_map/ppermute | solution.py:33
  9.2 0.6 compare_convert_fusion.live
  9.8 1.9 %cosine_bitcast_fusion = (f32[1,256,256]{2,1,0:T(8,128)S(1)}, f32[1,256,256]{2,1,0:T(8,128)S(1)}) fusion(f32[256,256]{1,0:T(8,128)} %param.19), kind=kLoop, calls=%fused_computation.2 | loop fusion | bytes 786432 | tf_op jit(solution)/shard_map/stack | solution.py:551
  11.6 0.8 pad_maximum_fusion.phase_kernel
  12.5 0.7 pad_add_fusion.1.here
  13.1 0.0 collective-permute-done.1.right_pos
  13.1 0.0 copy-start.2
  13.1 0.0 collective-permute-done.left_pos
  13.1 0.0 copy-start.3
  13.1 0.0 copy-done.1
  13.1 0.6 copy-done.2
  13.7 0.0 copy-done.3
  13.7 8.7 %shard_map.176 = (f32[6,2,256,256]{3,2,1,0:T(8,128)}, f32[6,2,256,128]{3,2,1,0:T(8,128)}, f32[6,2,256,128]{3,2,1,0:T(8,128)}) custom-call(s32[2]{0:T(128)} %pad_add_fusion.1.here, s32[7,2]{1,0:T(8,128)} %copy-done.3, s32[7,2]{1,0:T(8,128)} %copy-done.2, s32[7,2]{1,0:T(8,128)} %copy-done.1, f32[2,4096,256]{2,1,0:T(8,128)} %bitcast.12), custom_call_target="tpu_custom_call" | custom-call | tf_op jit(solution)/shard_map/pallas_call | solution.py:536
  22.4 141.5 %shard_map.177 = (f32[6,2,256,256]{3,2,1,0:T(8,128)}, f32[6,2,256,256]{3,2,1,0:T(8,128)}, f32[6,2,256,128]{3,2,1,0:T(8,128)}, f32[6,2,256,128]{3,2,1,0:T(8,128)}) custom-call(f32[6]{0:T(128)} %compare_convert_fusion.live, f32[6,2,256,128]{3,2,1,0:T(8,128)} %get-tuple-element.9.to_left, f32[6,2,256,128]{3,2,1,0:T(8,128)} %get-tuple-element.10.to_right, ...), custom_call_target="tpu_custom_call" | custom-call | tf_op jit(solution)/shard_map/pallas_call | solution.py:556
  163.9 0.0 copy-start
  163.9 10.3 %shard_map.178 = f32[2,4096,256]{2,1,0:T(8,128)} custom-call(s32[7,2]{1,0:T(8,128)} %copy-done.3, s32[7,2]{1,0:T(8,128)} %copy-done.2, s32[7,2]{1,0:T(8,128)} %copy-done.1, f32[6,2,256,256]{3,2,1,0:T(8,128)} %get-tuple-element.13.contrib, f32[6,2,256,128]{3,2,1,0:T(8,128)} %get-tuple-element.14.from_left, f32[6,2,256,128]{3,2,1,0:T(8,128)} %get-tuple-element.15.from_right), custom_call_target="tpu_custom_call" | custom-call | tf_op jit(solution)/shard_map/pallas_call | solution.py:586
  174.3 0.0 copy-done
  174.3 1.7 copy.28
Async XLA Ops:
  2.1 11.1 %copy-start.1 = (s32[7,2]{1,0:T(8,128)}, s32[7,2]{1,0:T(8,128)S(1)}, u32[]{:S(2)}) copy-start(s32[7,2]{1,0:T(8,128)S(1)} %pad_add_fusion.own_pos) | copy-start | bytes 172
  2.1 11.1 %collective-permute-start.1 = (s32[7,2]{1,0:T(8,128)S(1)}, s32[7,2]{1,0:T(8,128)S(1)}, u32[]{:S(2)}, u32[]{:S(2)}) collective-permute-start(s32[7,2]{1,0:T(8,128)S(1)} %pad_add_fusion.own_pos), channel_id=1, source_target_pairs={{1,0},{2,1},{3,2},{4,3},{5,4},{6,5},{7,6},{9,8},{10,9},{11,10},{12... | collective-permute-start | bytes 176 | tf_op jit(solution)/shard_map/ppermute | solution.py:33
  4.6 8.5 %collective-permute-start = (s32[7,2]{1,0:T(8,128)S(1)}, s32[7,2]{1,0:T(8,128)S(1)}, u32[]{:S(2)}, u32[]{:S(2)}) collective-permute-start(s32[7,2]{1,0:T(8,128)S(1)} %pad_add_fusion.own_pos), channel_id=1, source_target_pairs={{0,1},{1,2},{2,3},{3,4},{4,5},{5,6},{6,7},{8,9},{9,10},{10,11},{11... | collective-permute-start | bytes 176 | tf_op jit(solution)/shard_map/ppermute | solution.py:33
  13.1 0.6 copy-start.2
  13.1 0.6 copy-start.3
  163.9 10.4 %copy-start = (f32[6,2,256,256]{3,2,1,0:T(8,128)S(1)}, f32[6,2,256,256]{3,2,1,0:T(8,128)}, u32[]{:S(2)}) copy-start(f32[6,2,256,256]{3,2,1,0:T(8,128)} %get-tuple-element.12) | copy-start | bytes 9437188

commit v2 on v1

v2 whole, which is shorter than its diff:
```python
import functools
import math

import jax
import jax.numpy as jnp
import numpy as np
from jax import lax
from jax.experimental import pallas as pl
from jax.experimental.pallas import tpu as pltpu
from jax.sharding import PartitionSpec as P

RIM = 128
PAD = 8
MESH = pl.DeviceIdType.MESH
MIB = 1024 * 1024
EXTRACT_VMEM = 62 * MIB
PIPELINE_VMEM = 62 * MIB
GATHER_VMEM = 62 * MIB


def params(limit, **kw):
    return pltpu.CompilerParams(vmem_limit_bytes=limit, **kw)


def vmem():
    return pl.BlockSpec(memory_space=pltpu.VMEM)


def smem():
    return pl.BlockSpec(memory_space=pltpu.SMEM)


def shift(value, axis, by):
    count = lax.axis_size(axis)
    pairs = [(i, i + by) for i in range(count) if 0 <= i + by < count]
    return lax.ppermute(value, axis, pairs)


def make_tables(extent):
    half = extent // 2
    indices = np.arange(extent)
    angles = (indices[:, None] * indices[None, :] % extent) * (2.0 * math.pi / extent)
    cosine = (np.cos(angles) / math.sqrt(extent)).astype(np.float32)
    sine = (np.sin(angles) / math.sqrt(extent)).astype(np.float32)
    tables = []
    for parity in range(2):
        c, s = cosine[parity::2, :half], sine[parity::2, :half]
        block = np.block([[c, s], [-s, c]])
        for matrix in (block, block.T):
            hi = matrix.astype(jnp.bfloat16)
            lo = (matrix - hi.astype(np.float32)).astype(jnp.bfloat16)
            tables += [jnp.asarray(hi), jnp.asarray(lo)]
    order = np.concatenate([indices[0::2], indices[1::2]])
    sort = (order[:, None] == indices[None, :]).astype(jnp.bfloat16)
    return tables + [jnp.asarray(sort), jnp.asarray(np.ascontiguousarray(sort.T))]


def aligned(row, limit):
    base = jnp.minimum(row // PAD * PAD, limit)
    return pl.multiple_of(base, PAD), row - base


def extract_kernel(left_pos, right_pos, own_pos, trans, own, to_left, to_right,
                   buf_left, buf_right, buf_own, out_left, out_right, out_own, sem_in, sem_out):
    t = lax.axis_index("tile")
    end = lax.axis_size("tile") - 1
    slots, _, extent, _ = own.shape
    rows, cols = trans.shape[1:]
    tall = extent + PAD
    slack = cols + 2 * RIM - extent
    jobs = (
        (left_pos, buf_left, 0, RIM, out_left, to_left),
        (right_pos, buf_right, cols - RIM, RIM, out_right, to_right),
        (own_pos, buf_own, 0, cols, out_own, own),
    )

    def fetch(j, s):
        pos, buf, start, width = jobs[j][:4]
        base, off = aligned(pos[0, s], rows - tall)
        src = trans.at[:, pl.ds(base, tall), pl.ds(start, width)]
        return pltpu.make_async_copy(src, buf.at[s], sem_in.at[j, s]), off

    def flush(j, s):
        return pltpu.make_async_copy(jobs[j][4].at[s], jobs[j][5].at[s], sem_out.at[j, s])

    for s in range(slots):
        for j in range(3):
            fetch(j, s)[0].start()

    def columns(width):
        return lax.broadcasted_iota(jnp.int32, (extent, width), 1)

    def load(j, s, p, off, turn):
        value = pltpu.roll(jobs[j][1][s, p], (tall - off) % tall, 0)[:extent]
        return pltpu.roll(value, turn, 1)

    def body(s, carry):
        one, off = fetch(0, s)
        one.wait()
        short = slack - left_pos[1, s]
        at = columns(RIM) - short
        good = (at >= 0) & (at + 1 <= left_pos[1, slots])
        for p in range(2):
            out_left[s, p] = jnp.where(good, load(0, s, p, off, short % RIM), 0.0)
        flush(0, s).start()
        one, off = fetch(1, s)
        one.wait()
        col = right_pos[1, s]
        at = columns(RIM) + col
        good = (at < RIM) & (RIM - at <= right_pos[0, slots])
        for p in range(2):
            out_right[s, p] = jnp.where(good, load(1, s, p, off, (cols - col) % RIM), 0.0)
        flush(1, s).start()
        one, off = fetch(2, s)
        one.wait()
        col = own_pos[1, s]
        at = columns(extent) + col
        middle = (at >= RIM) & (at < RIM + cols)
        left_ok = (t > 0) & (at < RIM) & (RIM - at <= own_pos[0, slots])
        right_ok = (t < end) & (at >= RIM + cols) & (at - RIM - cols + 1 <= own_pos[1, slots])
        rim = left_ok | right_ok
        for p in range(2):
            value = load(2, s, p, off, (cols + RIM - col) % cols)
            out_own[s, p] = jnp.where(middle, value, jnp.where(rim, 0.0, 1.0 - p))
        flush(2, s).start()
        return carry

    lax.fori_loop(0, slots, body, 0)
    for s in range(slots):
        for j in range(3):
            flush(j, s).wait()


def gather_kernel(left_pos, right_pos, own_pos, contrib, from_left,
                  from_right, adjoint, grad, entry, acc, buf_own, buf_left, buf_right, buf_entry,
                  sem_in, sem_entry, sem_grad):
    slots, _, extent, _ = buf_own.shape
    rows, cols = acc.shape[1:]
    tall = extent + PAD
    slack = cols + 2 * RIM - extent
    jobs = ((contrib, buf_own), (from_left, buf_left), (from_right, buf_right))

    def fetch(j, s):
        return pltpu.make_async_copy(jobs[j][0].at[s], jobs[j][1].at[s], sem_in.at[j, s])

    for s in range(slots):
        for j in range(3):
            fetch(j, s).start()
    entry_in = pltpu.make_async_copy(adjoint, buf_entry, sem_entry.at[0])
    entry_out = pltpu.make_async_copy(buf_entry, entry, sem_entry.at[1])
    entry_in.start()
    acc[...] = jnp.zeros(acc.shape, acc.dtype)

    def columns(width):
        return lax.broadcasted_iota(jnp.int32, (extent, width), 1)

    def add(source, s, p, row, good, turn, start, width):
        base, off = aligned(row, rows - tall)
        value = jnp.where(good, pltpu.roll(source[s, p], turn, 1), 0.0)
        value = jnp.concatenate([value, jnp.zeros((PAD, width), jnp.float32)], axis=0)
        acc[p, pl.ds(base, tall), pl.ds(start, width)] += pltpu.roll(value, off, 0)

    def plane(p):
        def body(s, carry):
            if p == 0:
                for j in range(3):
                    fetch(j, s).wait()
            col = own_pos[1, s]
            at = columns(cols) + RIM - col
            good = (at >= 0) & (at < extent)
            add(buf_own, s, p, own_pos[0, s], good, (col + cols - RIM) % cols, 0, cols)
            short = slack - left_pos[1, s]
            at = columns(RIM)
            good = (at + short < RIM) & (at + 1 <= left_pos[1, slots])
            add(buf_left, s, p, left_pos[0, s], good, (cols - short) % RIM, 0, RIM)
            col = right_pos[1, s]
            good = (at >= col) & (RIM - at <= right_pos[0, slots])
            add(buf_right, s, p, right_pos[0, s], good, col % RIM, cols - RIM, RIM)
            return carry

        lax.fori_loop(0, slots, body, 0)

    def flush(p):
        return pltpu.make_async_copy(acc.at[p], grad.at[p], sem_grad.at[p])

    plane(0)
    flush(0).start()
    entry_in.wait()
    entry_out.start()
    plane(1)
    flush(1).start()
    entry_out.wait()
    flush(0).wait()
    flush(1).wait()


def pipeline_kernel(sections, tiles, counts, own, to_left, to_right, hbm_probe, hbm_phase, hbm_measured,
                    ef_hi, ef_lo, ei_hi, ei_lo, of_hi, of_lo, oi_hi, oi_lo, sort, unsort,
                    adjoint_out, contrib_out, from_left, from_right,
                    probe, phase, measured,
                    windows, left_rim, right_rim, arrived, leaving, backed, adjoint, contrib,
                    lefts, rights, turn, talls, wides, freq, spectrum,
                    sem_in, sem_own, sem_out, send_f, recv_f, send_b, recv_b,
                    send_rim, recv_rim, send_got, recv_got, token):
    g = lax.axis_index("cuts")
    t = lax.axis_index("tile")
    last = sections - 1
    mid = last - 1
    end = tiles - 1
    slots, _, extent, _ = windows.shape
    h = extent // 2
    partner = t + 1 - 2 * (t % 2)

    loads = [
        pltpu.make_async_copy(src, dst, sem_in.at[i])
        for i, (src, dst) in enumerate(
            ((hbm_phase, phase), (hbm_probe, probe), (hbm_measured, measured)))
    ]

    def own_part(s):
        return pltpu.make_async_copy(own.at[s], windows.at[s], sem_own.at[s])

    barrier = pltpu.get_barrier_semaphore()

    @pl.when(g > 0)
    def _():
        pl.semaphore_signal(barrier, inc=1, device_id={"cuts": g - 1}, device_id_type=MESH)

    @pl.when(g < last)
    def _():
        pl.semaphore_signal(barrier, inc=1, device_id={"cuts": g + 1}, device_id_type=MESH)

    @pl.when(t > 0)
    def _():
        pl.semaphore_signal(barrier, inc=1, device_id={"tile": t - 1}, device_id_type=MESH)

    @pl.when(t < end)
    def _():
        pl.semaphore_signal(barrier, inc=1, device_id={"tile": t + 1}, device_id_type=MESH)

    def exact(x, y):
        return jnp.dot(x, y, preferred_element_type=jnp.float32)

    def each(action):
        def body(s, carry):
            action(s)
            return carry

        lax.fori_loop(0, slots, body, 0)

    for load in loads:
        load.start()
    each(lambda s: own_part(s).start())

    forms = ((ef_hi, ef_lo, ei_hi, ei_lo), (of_hi, of_lo, oi_hi, oi_lo))
    for parity in range(2):
        fh, fl, ih, il = forms[parity]
        for inverse, (lh, ll, rh, rl) in enumerate(((fh, fl, ih, il), (ih, il, fh, fl))):
            at = 2 * inverse + parity
            lefts[at, :, :extent] = lh[...]
            lefts[at, :, extent : 2 * extent] = lh[...]
            lefts[at, :, 2 * extent :] = ll[...]
            rights[at, :extent] = rh[...]
            rights[at, extent : 2 * extent] = rh[...]
            rights[at, 2 * extent :] = rl[...]

    peers = (g + last - 1) // last + 1 - g // last + (t + end - 1) // end + 1 - t // end
    pl.semaphore_wait(barrier, peers)

    def rim_copy(side, s):
        src, dst = ((to_left, right_rim), (to_right, left_rim))[side]
        return pltpu.make_async_remote_copy(
            src_ref=src.at[s], dst_ref=dst.at[s], send_sem=send_rim.at[side, s],
            recv_sem=recv_rim.at[side, s], device_id={"tile": t + (-1, 1)[side]},
            device_id_type=MESH)

    def got_copy(side, s):
        start, dst = ((0, from_right), (extent - RIM, from_left))[side]
        return pltpu.make_async_remote_copy(
            src_ref=contrib.at[s, :, :, pl.ds(start, RIM)], dst_ref=dst.at[s],
            send_sem=send_got.at[side, s], recv_sem=recv_got.at[side, s],
            device_id={"tile": t + (-1, 1)[side]}, device_id_type=MESH)

    @pl.when(t > 0)
    def _():
        each(lambda s: rim_copy(0, s).start())

    @pl.when(t < end)
    def _():
        each(lambda s: rim_copy(1, s).start())

    @pl.when(t == 0)
    def _():
        left_rim[...] = jnp.zeros(left_rim.shape, left_rim.dtype)

    @pl.when(t == end)
    def _():
        right_rim[...] = jnp.zeros(right_rim.shape, right_rim.dtype)

    loads[0].wait()
    rest = phase[...]
    total = jnp.zeros((extent, extent), jnp.float32)
    for _ in range(3):
        part = rest.astype(jnp.bfloat16)
        rest = rest - part.astype(jnp.float32)
        total += exact(exact(sort[...], part).astype(jnp.bfloat16), unsort[...])
    turn[0] = jnp.cos(total)
    sine = jnp.sin(total)
    turn[1] = sine
    turn[2] = -sine
    loads[1].wait()
    loads[2].wait()

    def split(value):
        hi = value.astype(jnp.bfloat16)
        lo = (value - hi.astype(jnp.float32)).astype(jnp.bfloat16)
        return (hi, lo, hi)

    def put_tall(parity, p, value):
        for at, part in enumerate(split(value)):
            talls[parity, pl.ds(at * extent + p * h, h), :] = part

    def put_wide(parity, rows, p, value):
        n = value.shape[0]
        for at, part in enumerate(split(value)):
            wides[parity, pl.ds(rows, n), pl.ds(at * extent + p * h, h)] = part

    def left(at):
        return exact(lefts[at], talls[at % 2])

    def right(at):
        return exact(wides[at % 2], rights[at])

    def to_freq():
        for p in range(2):
            put_tall(0, p, spectrum[p, :h] + spectrum[p, h:])
            put_tall(1, p, spectrum[p, :h] - spectrum[p, h:])
        for block in range(2):
            half = left(block)
            for p in range(2):
                value = half[p * h : (p + 1) * h]
                put_wide(0, block * h, p, value[:, :h] + value[:, h:])
                put_wide(1, block * h, p, value[:, :h] - value[:, h:])
        for parity in range(2):
            freq[parity] = right(parity)

    def from_freq():
        u, v = right(2), right(3)
        for p in range(2):
            up, vp = u[:, p * h : (p + 1) * h], v[:, p * h : (p + 1) * h]
            plus, minus = up + vp, up - vp
            for parity in range(2):
                rows = slice(parity * h, (parity + 1) * h)
                both = jnp.concatenate([plus[rows], minus[rows]], axis=1)
                put_tall(parity, p, both)
        u, v = left(2), left(3)
        for p in range(2):
            up, vp = u[p * h : (p + 1) * h], v[p * h : (p + 1) * h]
            spectrum[p, :h] = up + vp
            spectrum[p, h:] = up - vp

    def send_forward(s, part):
        return pltpu.make_async_remote_copy(
            src_ref=leaving.at[s, part], dst_ref=arrived.at[s, part], send_sem=send_f.at[s, part],
            recv_sem=recv_f.at[s, part], device_id={"cuts": g + 1}, device_id_type=MESH)

    def send_backward(s):
        return pltpu.make_async_remote_copy(
            src_ref=adjoint.at[s], dst_ref=backed.at[s], send_sem=send_b.at[s],
            recv_sem=recv_b.at[s], device_id={"cuts": g - 1}, device_id_type=MESH)

    def send_window(s):
        return pltpu.make_async_remote_copy(
            src_ref=windows.at[s], dst_ref=backed.at[s], send_sem=send_b.at[s],
            recv_sem=recv_b.at[s], device_id={"cuts": g - 1}, device_id_type=MESH)

    def compose(s):
        own_part(s).wait()

        @pl.when(t < end)
        def _():
            rim_copy(0, s).wait_recv()

        @pl.when(t > 0)
        def _():
            rim_copy(1, s).wait_recv()

        for p in range(2):
            windows[s, p, :, :RIM] += left_rim[s, p]
            windows[s, p, :, extent - RIM :] += right_rim[s, p]

    def put_out(j, s):
        src, dst = ((adjoint, adjoint_out), (contrib, contrib_out))[j]
        return pltpu.make_async_copy(src.at[s], dst.at[s], sem_out.at[j, s])

    def product(w, x, s, sign):
        wr, wi = w[s, 0], w[s, 1]
        xr, xi = x
        spectrum[0] = wr * xr - sign * (wi * xi)
        spectrum[1] = wr * xi + sign * (wi * xr)

    @pl.when(g == last)
    def _():
        def body(s):
            compose(s)
            send_window(s).start()

        each(body)

    def event(s, op):
        @pl.when(op == 0)
        def _():
            @pl.when(g == 0)
            def _():
                arrived[s] = probe[...] * jnp.clip(counts[0] - s, 0, 1).astype(jnp.float32)

            @pl.when(g > 0)
            def _():
                send_forward(s, 0).wait_recv()
                send_forward(s, 1).wait_recv()

            @pl.when(g < last)
            def _():
                compose(s)

            product(windows, (arrived[s, 0], arrived[s, 1]), s, 1.0)

        @pl.when(op == 1)
        def _():
            send_window(s).wait_recv()
            product(backed, (spectrum[0], spectrum[1]), s, 1.0)

        @pl.when((op == 4) & (g < mid))
        def _():
            send_backward(s).wait_recv()
            spectrum[...] = backed[s]

        @pl.when((op == 4) & (g == mid))
        def _():
            product(backed, (spectrum[0], spectrum[1]), s, -1.0)

        to_freq()

        @pl.when(op == 2)
        def _():
            seen = exact(sort[...], measured[s]).astype(jnp.bfloat16)
            seen = exact(seen, unsort[...])
            for parity in range(2):
                fr, fi = freq[parity, :, :h], freq[parity, :, h:]
                residual = fr * fr + fi * fi - seen[:, parity * h : (parity + 1) * h]
                put_wide(parity, 0, 0, fr * residual)
                put_wide(parity, 0, 1, fi * residual)

        @pl.when(op != 2)
        def _():
            sine = 1 + op // 3
            for parity in range(2):
                cols = slice(parity * h, (parity + 1) * h)
                kr, ki = turn[0, :, cols], turn[sine, :, cols]
                xr, xi = freq[parity, :, :h], freq[parity, :, h:]
                put_wide(parity, 0, 0, kr * xr - ki * xi)
                put_wide(parity, 0, 1, kr * xi + ki * xr)

        from_freq()

        @pl.when((op == 0) & (g < last))
        def _():
            leaving[s] = spectrum[...]

            @pl.when((g == 0) & ((s > 0) | (t % 2 == 1)))
            def _():
                pl.semaphore_wait(token, 1)

            send_forward(s, 0).start()
            send_forward(s, 1).start()

            @pl.when(g == 0)
            def _():
                send_forward(s, 0).wait_send()

                @pl.when((s < slots - 1) | (t % 2 == 0))
                def _():
                    pl.semaphore_signal(token, inc=1, device_id={"tile": partner}, device_id_type=MESH)

        @pl.when(((op == 3) & (g == last)) | (op == 4))
        def _():
            tr, ti = spectrum[0], spectrum[1]
            wr, wi = windows[s, 0], windows[s, 1]
            adjoint[s, 0] = wr * tr + wi * ti
            adjoint[s, 1] = wr * ti - wi * tr

            @pl.when((g > 0) & (g < last))
            def _():
                send_backward(s).start()

            xr, xi = arrived[s, 0], arrived[s, 1]
            contrib[s, 0] = xr * tr + xi * ti
            contrib[s, 1] = xr * ti - xi * tr
            put_out(0, s).start()
            put_out(1, s).start()

            @pl.when(t > 0)
            def _():
                got_copy(0, s).start()

            @pl.when(t < end)
            def _():
                got_copy(1, s).start()

    lag = 2 * (mid - g)
    early = (g < mid).astype(jnp.int32)
    final = g // last
    ops = 5 - 3 * early - 2 * final
    count = (slots + early * lag) * ops

    def step(e, carry):
        k, part = e // ops, e % ops
        s = k - early * part * lag
        op = part + early * part * 3 + final * ((part + 1) // 2)

        @pl.when((s >= 0) & (s < slots))
        def _():
            event(s, op)

        return carry

    lax.fori_loop(0, count, step, 0)

    @pl.when(g < last)
    def _():
        each(lambda s: send_forward(s, 1).wait_send())

    @pl.when((g > 0) & (g < last))
    def _():
        each(lambda s: send_forward(s, 0).wait_send())
        each(lambda s: send_backward(s).wait_send())

    @pl.when(g == last)
    def _():
        each(lambda s: send_window(s).wait_send())

    @pl.when(t < end)
    def _():
        each(lambda s: got_copy(0, s).wait_recv())

    @pl.when(t > 0)
    def _():
        each(lambda s: got_copy(1, s).wait_recv())

    def finish(side):
        def body(s):
            rim_copy(side, s).wait_send()
            got_copy(side, s).wait_send()

        each(body)

    @pl.when(t > 0)
    def _():
        finish(0)

    @pl.when(t < end)
    def _():
        finish(1)

    each(lambda s: put_out(0, s).wait())
    each(lambda s: put_out(1, s).wait())


def on_device(probe_wave, transmission, kernel_phase, measured, counts, positions, widths):
    f32 = jnp.float32
    bf16 = jnp.bfloat16
    rows, cols = transmission.shape[2:]
    extent = probe_wave.shape[-1]
    slots = positions.shape[1]
    sections = lax.axis_size("cuts")
    tiles = lax.axis_size("tile")
    assert extent == cols and extent >= 2 * RIM and tiles % 2 == 0 and sections >= 2
    own_pos = jnp.concatenate([jnp.swapaxes(positions[0], 0, 1), widths.reshape(2, 1)], 1)
    right_pos = shift(own_pos, "tile", -1)
    left_pos = shift(own_pos, "tile", 1)
    sds = jax.ShapeDtypeStruct
    wave = sds((slots, 2, extent, extent), f32)
    rim = sds((slots, 2, extent, RIM), f32)
    waves = pltpu.VMEM(wave.shape, f32)
    rims = pltpu.VMEM(rim.shape, f32)
    hbm = pl.BlockSpec(memory_space=pl.ANY)
    dma = pltpu.SemaphoreType.DMA
    tall = extent + PAD
    own, to_left, to_right = pl.pallas_call(
        extract_kernel,
        out_shape=(wave, rim, rim),
        in_specs=[smem()] * 3 + [hbm],
        out_specs=(hbm,) * 3,
        scratch_shapes=[
            pltpu.VMEM((slots, 2, tall, RIM), f32),
            pltpu.VMEM((slots, 2, tall, RIM), f32),
            pltpu.VMEM((slots, 2, tall, cols), f32),
            rims, rims, waves,
            dma((3, slots)), dma((3, slots)),
        ],
        compiler_params=params(EXTRACT_VMEM),
    )(left_pos, right_pos, own_pos, transmission[0])
    adjoint, contrib, from_left, from_right = pl.pallas_call(
        functools.partial(pipeline_kernel, sections, tiles),
        out_shape=(wave, wave, rim, rim),
        in_specs=[smem()] + [hbm] * 6 + [vmem()] * 10,
        out_specs=(hbm,) * 4,
        scratch_shapes=[
            pltpu.VMEM((2, extent, extent), f32),
            pltpu.VMEM((extent, extent), f32),
            pltpu.VMEM((slots, extent, extent), bf16),
            waves, rims, rims,
            waves, waves, waves, waves, waves,
            pltpu.VMEM((4, extent, 3 * extent), bf16),
            pltpu.VMEM((4, 3 * extent, extent), bf16),
            pltpu.VMEM((3, extent, extent), f32),
            pltpu.VMEM((2, 3 * extent, extent), bf16),
            pltpu.VMEM((2, extent, 3 * extent), bf16),
            pltpu.VMEM((2, extent, extent), f32),
            pltpu.VMEM((2, extent, extent), f32),
            dma((3,)),
            dma((slots,)),
            dma((2, slots)),
            dma((slots, 2)), dma((slots, 2)),
            dma((slots,)), dma((slots,)),
            dma((2, slots)), dma((2, slots)),
            dma((2, slots)), dma((2, slots)),
            pltpu.SemaphoreType.REGULAR,
        ],
        compiler_params=params(PIPELINE_VMEM, collective_id=0, has_side_effects=True),
    )(counts, own, to_left, to_right, probe_wave, kernel_phase, measured[0], *make_tables(extent))
    grad, entry = pl.pallas_call(
        gather_kernel,
        out_shape=(sds((2, rows, cols), f32), wave),
        in_specs=[smem()] * 3 + [hbm] * 4,
        out_specs=(hbm, hbm),
        scratch_shapes=[
            pltpu.VMEM((2, rows, cols), f32), waves, rims, rims, waves,
            dma((3, slots)), dma((2,)), dma((2,)),
        ],
        compiler_params=params(GATHER_VMEM),
    )(left_pos, right_pos, own_pos, contrib, from_left, from_right, adjoint)
    return (entry[None, None], grad[None])


def solution(mesh):
    return jax.shard_map(
        on_device,
        mesh=mesh,
        in_specs=(
            P(),
            P("cuts", None, None, "tile"),
            P(),
            P("tile", None, None, None),
            P("tile"),
            P("tile", None, None),
            P("tile", None),
        ),
        out_specs=(P("cuts", "tile", None, None, None, None), P("cuts", None, None, "tile")),
        check_vma=False,
    )
```

time: 176 us -> 164 us (0.932)
  Pallas kernels: 161 us -> 153 us
  local copies, waits for them, and re-layouts: 4.86 us -> 1.32 us
  other arithmetic: 2.73 us -> 0.75 us
    pallas_call x2, Pallas kernels: 152 us -> 147 us  [the longest x1 138 us: on_device(): pl.pallas_call(functools.partial(pipeline_kernel, sections, tiles), out_s...]
    pallas_call x1, Pallas kernels: 8.66 us -> 6.6 us  [on_device(): pl.pallas_call(extract_kernel, out_shape=(wave, rim, rim), in_specs=[smem...]
    another operation x1 -> x0, local copies, waits for them, and re-layouts: 1.85 us -> none  [on_device(): phase_kernel = jnp.stack([jnp.cos(kernel_phase), jnp.sin(kernel_phase)], 0)]
  transfers between devices with their start and end apart: 2 -> 2, of which waited for: 0 -> 0; matrix products, arithmetic and copies ran while one was open for 2% -> 0% of each run, Pallas kernels for 0% -> 0%
where the time goes in v2:
time: 164 us; the launch traced here: 163 us
  Pallas kernels  153 us (93%)
  starting transfers between devices  6.45 us (4%)
    pallas_call x1, Pallas kernels, on_device(): pl.pallas_call(functools.partial(pipeline_kernel, sections, tiles), out_s...  138 us
    pallas_call x1, Pallas kernels, on_device(): pl.pallas_call(gather_kernel, out_shape=(sds((2, rows, cols), f32), wave)...  8.79 us
    pallas_call x1, Pallas kernels, on_device(): pl.pallas_call(extract_kernel, out_shape=(wave, rim, rim), in_specs=[smem...  6.6 us
    ppermute x2, starting transfers between devices, shift(): return lax.ppermute(value, axis, pairs)  6.45 us
  transfers between devices with their start and end apart: 2, of which 0 were waited for; matrix products, arithmetic and copies ran while one was open for 0% of the time, Pallas kernels for 0%

profile of v2, /device:TPU:3, one launch (start us, length us, event | category | flops | bytes accessed | tf_op | source)
XLA Modules:
  0.0 163.0 jit_solution(16053510532444095130)
XLA Ops:
  0.6 0.7 copy.19
  1.4 0.8 pad_add_fusion.own_pos
  2.1 0.0 copy-start
  2.1 2.6 %collective-permute-start.1 = (s32[2,7]{1,0:T(2,128)S(1)}, s32[2,7]{1,0:T(2,128)S(1)}, u32[]{:S(2)}, u32[]{:S(2)}) collective-permute-start(s32[2,7]{1,0:T(2,128)S(1)} %pad_add_fusion.own_pos), channel_id=1, source_target_pairs={{1,0},{2,1},{3,2},{4,3},{5,4},{6,5},{7,6},{9,8},{10,9},{11,10},{12... | collective-permute-start | bytes 176 | tf_op jit(solution)/shard_map/ppermute | solution.py:36
  4.7 3.9 %collective-permute-start = (s32[2,7]{1,0:T(2,128)S(1)}, s32[2,7]{1,0:T(2,128)S(1)}, u32[]{:S(2)}, u32[]{:S(2)}) collective-permute-start(s32[2,7]{1,0:T(2,128)S(1)} %pad_add_fusion.own_pos), channel_id=1, source_target_pairs={{0,1},{1,2},{2,3},{3,4},{4,5},{5,6},{6,7},{8,9},{9,10},{10,11},{11... | collective-permute-start | bytes 176 | tf_op jit(solution)/shard_map/ppermute | solution.py:36
  9.2 0.0 collective-permute-done.1.right_pos
  9.2 0.0 copy-start.1
  9.3 0.0 collective-permute-done.left_pos
  9.3 0.0 copy-start.2
  9.3 0.0 copy-done
  9.3 0.5 copy-done.1
  9.8 0.0 copy-done.2
  9.9 6.6 %shard_map.176 = (f32[6,2,256,256]{3,2,1,0:T(8,128)}, f32[6,2,256,128]{3,2,1,0:T(8,128)}, f32[6,2,256,128]{3,2,1,0:T(8,128)}) custom-call(s32[2,7]{1,0:T(2,128)} %copy-done.2, s32[2,7]{1,0:T(2,128)} %copy-done.1, s32[2,7]{1,0:T(2,128)} %copy-done, f32[2,4096,256]{2,1,0:T(8,128)} %bitcast.8), custom_call_target="tpu_custom_call" | custom-call | tf_op jit(solution)/shard_map/pallas_call | solution.py:589
  16.5 137.7 %shard_map.177 = (f32[6,2,256,256]{3,2,1,0:T(8,128)}, f32[6,2,256,256]{3,2,1,0:T(8,128)}, f32[6,2,256,128]{3,2,1,0:T(8,128)}, f32[6,2,256,128]{3,2,1,0:T(8,128)}) custom-call(s32[1]{0:T(128)S(6)} %copy.20.counts, f32[6,2,256,256]{3,2,1,0:T(8,128)} %get-tuple-element.11.own, f32[6,2,256,128]{3,2,1,0:T(8,128)} %get-tuple-element.12.to_left, ...), custom_call_target="tpu_custom_call" | custom-call | tf_op jit(solution)/shard_map/pallas_call | solution.py:603
  154.2 8.8 %shard_map.178 = (f32[2,4096,256]{2,1,0:T(8,128)}, f32[6,2,256,256]{3,2,1,0:T(8,128)}) custom-call(s32[2,7]{1,0:T(2,128)} %copy-done.2, s32[2,7]{1,0:T(2,128)} %copy-done.1, s32[2,7]{1,0:T(2,128)} %copy-done, f32[6,2,256,256]{3,2,1,0:T(8,128)} %get-tuple-element.14.contrib, f32[6,2,256,128]{3,2,1,0:T(8,128)} %get-tuple-element.15.from_left, ...), custom_call_target="tpu_custom_call" | custom-call | tf_op jit(solution)/shard_map/pallas_call | solution.py:632
Async XLA Ops:
  2.1 7.2 %copy-start = (s32[2,7]{1,0:T(2,128)}, s32[2,7]{1,0:T(2,128)S(1)}, u32[]{:S(2)}) copy-start(s32[2,7]{1,0:T(2,128)S(1)} %pad_add_fusion.own_pos) | copy-start | bytes 172
  2.1 7.1 %collective-permute-start.1 = (s32[2,7]{1,0:T(2,128)S(1)}, s32[2,7]{1,0:T(2,128)S(1)}, u32[]{:S(2)}, u32[]{:S(2)}) collective-permute-start(s32[2,7]{1,0:T(2,128)S(1)} %pad_add_fusion.own_pos), channel_id=1, source_target_pairs={{1,0},{2,1},{3,2},{4,3},{5,4},{6,5},{7,6},{9,8},{10,9},{11,10},{12... | collective-permute-start | bytes 176 | tf_op jit(solution)/shard_map/ppermute | solution.py:36
  4.7 4.6 %collective-permute-start = (s32[2,7]{1,0:T(2,128)S(1)}, s32[2,7]{1,0:T(2,128)S(1)}, u32[]{:S(2)}, u32[]{:S(2)}) collective-permute-start(s32[2,7]{1,0:T(2,128)S(1)} %pad_add_fusion.own_pos), channel_id=1, source_target_pairs={{0,1},{1,2},{2,3},{3,4},{4,5},{5,6},{6,7},{8,9},{9,10},{10,11},{11... | collective-permute-start | bytes 176 | tf_op jit(solution)/shard_map/ppermute | solution.py:36
  9.2 0.6 copy-start.1
  9.3 0.6 copy-start.2

commit v3 on v2

--- a/solution.py
+++ b/solution.py
@@ -194,13 +194,41 @@
     flush(1).wait()
 
 
+ENTER, BEYOND, WHOLE, BACK, OFFER, RELAY = range(1, 7)
+
+
+def schedule(g, last, slots):
+    mid, alone = last - 1, slots - 1
+    relays = [(0, RELAY, m) for m in range(g + 1, last + 1)]
+    plan = [(0, OFFER, g)] * (0 < g < last)
+    if g >= mid:
+        return plan + relays + [(s, WHOLE, g) for s in range(slots)]
+    lag = 2 * (mid - g)
+    done = 0
+    for k in range(slots):
+        plan += [(k, ENTER, g)]
+        if g > 0 and relays:
+            plan += [relays.pop(0)]
+        if k >= lag:
+            plan += [(done, BACK, g)]
+            done += 1
+    while done < alone - 2:
+        plan += [(done, BACK, g)]
+        done += 1
+    plan += relays + [(alone, BEYOND, g)]
+    while done < alone:
+        plan += [(done, BACK, g)]
+        done += 1
+    return plan
+
+
 def pipeline_kernel(sections, tiles, counts, own, to_left, to_right, hbm_probe, hbm_phase, hbm_measured,
                     ef_hi, ef_lo, ei_hi, ei_lo, of_hi, of_lo, oi_hi, oi_lo, sort, unsort,
                     adjoint_out, contrib_out, from_left, from_right,
                     probe, phase, measured,
                     windows, left_rim, right_rim, arrived, leaving, backed, adjoint, contrib,
-                    lefts, rights, turn, talls, wides, freq, spectrum,
-                    sem_in, sem_own, sem_out, send_f, recv_f, send_b, recv_b,
+                    lefts, rights, turn, talls, wides, spectrum,
+                    sem_in, sem_own, sem_out, send_f, recv_f, send_b, recv_b, send_far, recv_far,
                     send_rim, recv_rim, send_got, recv_got, token):
     g = lax.axis_index("cuts")
     t = lax.axis_index("tile")
@@ -210,6 +238,7 @@
     slots, _, extent, _ = windows.shape
     h = extent // 2
     partner = t + 1 - 2 * (t % 2)
+    alone = slots - 1
 
     loads = [
         pltpu.make_async_copy(src, dst, sem_in.at[i])
@@ -251,6 +280,9 @@
     for load in loads:
         load.start()
     each(lambda s: own_part(s).start())
+
+    def turn_of(i):
+        return (i + alone * ((g + last - 1) // last)) % slots
 
     forms = ((ef_hi, ef_lo, ei_hi, ei_lo), (of_hi, of_lo, oi_hi, oi_lo))
     for parity in range(2):
@@ -281,13 +313,18 @@
             send_sem=send_got.at[side, s], recv_sem=recv_got.at[side, s],
             device_id={"tile": t + (-1, 1)[side]}, device_id_type=MESH)
 
-    @pl.when(t > 0)
-    def _():
-        each(lambda s: rim_copy(0, s).start())
-
-    @pl.when(t < end)
-    def _():
-        each(lambda s: rim_copy(1, s).start())
+    def rims_start(i):
+        s = turn_of(i)
+
+        @pl.when(t > 0)
+        def _():
+            rim_copy(0, s).start()
+
+        @pl.when(t < end)
+        def _():
+            rim_copy(1, s).start()
+
+    each(rims_start)
 
     @pl.when(t == 0)
     def _():
@@ -331,10 +368,38 @@
     def right(at):
         return exact(wides[at % 2], rights[at])
 
-    def to_freq():
+    def halves(load):
+        upper, lower = load(slice(0, h)), load(slice(h, extent))
         for p in range(2):
-            put_tall(0, p, spectrum[p, :h] + spectrum[p, h:])
-            put_tall(1, p, spectrum[p, :h] - spectrum[p, h:])
+            put_tall(0, p, upper[p] + lower[p])
+            put_tall(1, p, upper[p] - lower[p])
+
+    def plain(ref, *at):
+        def load(rows):
+            return [ref[(*at, p, rows)] for p in range(2)]
+
+        return load
+
+    def through(w, w_at, x, x_at, sign):
+        def load(rows):
+            wr, wi = w[w_at, 0, rows], w[w_at, 1, rows]
+            xr, xi = x[(*x_at, 0, rows)], x[(*x_at, 1, rows)]
+            if sign > 0:
+                return [wr * xr - wi * xi, wr * xi + wi * xr]
+            return [wr * xr + wi * xi, wr * xi - wi * xr]
+
+        return load
+
+    def turned(sine):
+        def middle(parity, xr, xi):
+            cols = slice(parity * h, (parity + 1) * h)
+            kr, ki = turn[0, :, cols], turn[sine, :, cols]
+            return kr * xr - ki * xi, kr * xi + ki * xr
+
+        return middle
+
+    def transform(load, middle):
+        halves(load)
         for block in range(2):
             half = left(block)
             for p in range(2):
@@ -342,17 +407,16 @@
                 put_wide(0, block * h, p, value[:, :h] + value[:, h:])
                 put_wide(1, block * h, p, value[:, :h] - value[:, h:])
         for parity in range(2):
-            freq[parity] = right(parity)
-
-    def from_freq():
+            value = right(parity)
+            for p, part in enumerate(middle(parity, value[:, :h], value[:, h:])):
+                put_wide(parity, 0, p, part)
         u, v = right(2), right(3)
         for p in range(2):
             up, vp = u[:, p * h : (p + 1) * h], v[:, p * h : (p + 1) * h]
             plus, minus = up + vp, up - vp
             for parity in range(2):
                 rows = slice(parity * h, (parity + 1) * h)
-                both = jnp.concatenate([plus[rows], minus[rows]], axis=1)
-                put_tall(parity, p, both)
+                put_tall(parity, p, jnp.concatenate([plus[rows], minus[rows]], axis=1))
         u, v = left(2), left(3)
         for p in range(2):
             up, vp = u[p * h : (p + 1) * h], v[p * h : (p + 1) * h]
@@ -374,6 +438,19 @@
             src_ref=windows.at[s], dst_ref=backed.at[s], send_sem=send_b.at[s],
             recv_sem=recv_b.at[s], device_id={"cuts": g - 1}, device_id_type=MESH)
 
+    def far_at(m):
+        return slots + m - 1
+
+    def send_own_far():
+        return pltpu.make_async_remote_copy(
+            src_ref=windows.at[alone], dst_ref=backed.at[far_at(g)], send_sem=send_far.at[g],
+            recv_sem=recv_far.at[g], device_id={"cuts": g - 1}, device_id_type=MESH)
+
+    def send_far_on(m):
+        return pltpu.make_async_remote_copy(
+            src_ref=backed.at[far_at(m)], dst_ref=backed.at[far_at(m)], send_sem=send_far.at[m],
+            recv_sem=recv_far.at[m], device_id={"cuts": g - 1}, device_id_type=MESH)
+
     def compose(s):
         own_part(s).wait()
 
@@ -393,77 +470,39 @@
         src, dst = ((adjoint, adjoint_out), (contrib, contrib_out))[j]
         return pltpu.make_async_copy(src.at[s], dst.at[s], sem_out.at[j, s])
 
-    def product(w, x, s, sign):
-        wr, wi = w[s, 0], w[s, 1]
-        xr, xi = x
-        spectrum[0] = wr * xr - sign * (wi * xi)
-        spectrum[1] = wr * xi + sign * (wi * xr)
-
     @pl.when(g == last)
     def _():
-        def body(s):
+        def body(i):
+            s = turn_of(i)
             compose(s)
-            send_window(s).start()
+
+            @pl.when(s == alone)
+            def _():
+                send_own_far().start()
+
+            @pl.when(s < alone)
+            def _():
+                send_window(s).start()
 
         each(body)
 
-    def event(s, op):
-        @pl.when(op == 0)
-        def _():
-            @pl.when(g == 0)
-            def _():
-                arrived[s] = probe[...] * jnp.clip(counts[0] - s, 0, 1).astype(jnp.float32)
-
-            @pl.when(g > 0)
-            def _():
-                send_forward(s, 0).wait_recv()
-                send_forward(s, 1).wait_recv()
-
-            @pl.when(g < last)
-            def _():
-                compose(s)
-
-            product(windows, (arrived[s, 0], arrived[s, 1]), s, 1.0)
-
-        @pl.when(op == 1)
-        def _():
-            send_window(s).wait_recv()
-            product(backed, (spectrum[0], spectrum[1]), s, 1.0)
-
-        @pl.when((op == 4) & (g < mid))
-        def _():
-            send_backward(s).wait_recv()
-            spectrum[...] = backed[s]
-
-        @pl.when((op == 4) & (g == mid))
-        def _():
-            product(backed, (spectrum[0], spectrum[1]), s, -1.0)
-
-        to_freq()
-
-        @pl.when(op == 2)
-        def _():
-            seen = exact(sort[...], measured[s]).astype(jnp.bfloat16)
-            seen = exact(seen, unsort[...])
-            for parity in range(2):
-                fr, fi = freq[parity, :, :h], freq[parity, :, h:]
-                residual = fr * fr + fi * fi - seen[:, parity * h : (parity + 1) * h]
-                put_wide(parity, 0, 0, fr * residual)
-                put_wide(parity, 0, 1, fi * residual)
-
-        @pl.when(op != 2)
-        def _():
-            sine = 1 + op // 3
-            for parity in range(2):
-                cols = slice(parity * h, (parity + 1) * h)
-                kr, ki = turn[0, :, cols], turn[sine, :, cols]
-                xr, xi = freq[parity, :, :h], freq[parity, :, h:]
-                put_wide(parity, 0, 0, kr * xr - ki * xi)
-                put_wide(parity, 0, 1, kr * xi + ki * xr)
-
-        from_freq()
-
-        @pl.when((op == 0) & (g < last))
+    def enter(s):
+        @pl.when(g == 0)
+        def _():
+            arrived[s] = probe[...] * jnp.clip(counts[0] - s, 0, 1).astype(jnp.float32)
+
+        @pl.when(g > 0)
+        def _():
+            send_forward(s, 0).wait_recv()
+            send_forward(s, 1).wait_recv()
+
+        @pl.when((g < last) & ((g == 0) | (s < alone)))
+        def _():
+            compose(s)
+
+        transform(through(windows, s, arrived, (s,), 1), turned(1))
+
+        @pl.when(g < last)
         def _():
             leaving[s] = spectrum[...]
 
@@ -482,49 +521,119 @@
                 def _():
                     pl.semaphore_signal(token, inc=1, device_id={"tile": partner}, device_id_type=MESH)
 
-        @pl.when(((op == 3) & (g == last)) | (op == 4))
-        def _():
-            tr, ti = spectrum[0], spectrum[1]
-            wr, wi = windows[s, 0], windows[s, 1]
-            adjoint[s, 0] = wr * tr + wi * ti
-            adjoint[s, 1] = wr * ti - wi * tr
-
-            @pl.when((g > 0) & (g < last))
+    def beyond(s):
+        later = last - g
+
+        @pl.when((g == mid) & (s < alone))
+        def _():
+            send_window(s).wait_recv()
+
+        @pl.when(g < mid)
+        def _():
+            spectrum[...] = leaving[s]
+
+        def onward(i, carry):
+            spot = jnp.where(s == alone, far_at(g + 1 + i), s)
+            transform(through(backed, spot, spectrum, (), 1), turned(1))
+            return carry
+
+        lax.fori_loop(0, later, onward, 0)
+        seen = exact(sort[...], measured[s]).astype(jnp.bfloat16)
+        seen = exact(seen, unsort[...])
+
+        def detected(parity, xr, xi):
+            residual = xr * xr + xi * xi - seen[:, parity * h : (parity + 1) * h]
+            return xr * residual, xi * residual
+
+        transform(plain(spectrum), detected)
+        transform(plain(spectrum), turned(2))
+
+        def homeward(i, carry):
+            spot = jnp.where(s == alone, far_at(last - i), s)
+            transform(through(backed, spot, spectrum, (), -1), turned(2))
+            return carry
+
+        lax.fori_loop(0, later, homeward, 0)
+
+    def back(s):
+        send_backward(s).wait_recv()
+        transform(plain(backed, s), turned(2))
+
+    def finish_slot(s):
+        tr, ti = spectrum[0], spectrum[1]
+        wr, wi = windows[s, 0], windows[s, 1]
+        adjoint[s, 0] = wr * tr + wi * ti
+        adjoint[s, 1] = wr * ti - wi * tr
+
+        @pl.when((g > 0) & (g < last) & (s < alone))
+        def _():
+            send_backward(s).start()
+
+        xr, xi = arrived[s, 0], arrived[s, 1]
+        contrib[s, 0] = xr * tr + xi * ti
+        contrib[s, 1] = xr * ti - xi * tr
+
+        @pl.when(t > 0)
+        def _():
+            got_copy(0, s).start()
+
+        @pl.when(t < end)
+        def _():
+            got_copy(1, s).start()
+
+        put_out(0, s).start()
+        put_out(1, s).start()
+
+    plans = [schedule(here, last, slots) for here in range(sections)]
+    width = max(len(plan) for plan in plans)
+
+    def step(e, carry):
+        code = jnp.int32(0)
+        for here, plan in enumerate(plans):
+            for at, (s, act, m) in enumerate(plan):
+                code = jnp.where((g == here) & (e == at), (s * 8 + act) * (sections + 1) + m + 1, code)
+        m, rest = code % (sections + 1) - 1, code // (sections + 1)
+        act, s = rest % 8, rest // 8
+
+        @pl.when((act == ENTER) | (act == WHOLE))
+        def _():
+            enter(s)
+
+        @pl.when((act == BEYOND) | (act == WHOLE))
+        def _():
+            beyond(s)
+
+        @pl.when(act == BACK)
+        def _():
+            back(s)
+
+        @pl.when((act == BEYOND) | (act == WHOLE) | (act == BACK))
+        def _():
+            finish_slot(s)
+
+        @pl.when(act == OFFER)
+        def _():
+            compose(alone)
+            send_own_far().start()
+
+        @pl.when(act == RELAY)
+        def _():
+            send_far_on(m).wait_recv()
+
+            @pl.when(g > 0)
             def _():
-                send_backward(s).start()
-
-            xr, xi = arrived[s, 0], arrived[s, 1]
-            contrib[s, 0] = xr * tr + xi * ti
-            contrib[s, 1] = xr * ti - xi * tr
-            put_out(0, s).start()
-            put_out(1, s).start()
-
-            @pl.when(t > 0)
-            def _():
-                got_copy(0, s).start()
-
-            @pl.when(t < end)
-            def _():
-                got_copy(1, s).start()
-
-    lag = 2 * (mid - g)
-    early = (g < mid).astype(jnp.int32)
-    final = g // last
-    ops = 5 - 3 * early - 2 * final
-    count = (slots + early * lag) * ops
-
-    def step(e, carry):
-        k, part = e // ops, e % ops
-        s = k - early * part * lag
-        op = part + early * part * 3 + final * ((part + 1) // 2)
-
-        @pl.when((s >= 0) & (s < slots))
-        def _():
-            event(s, op)
+                send_far_on(m).start()
 
         return carry
 
-    lax.fori_loop(0, count, step, 0)
+    lax.fori_loop(0, width, step, 0)
+
+    def all_but_lone(action):
+        def body(s, carry):
+            action(s)
+            return carry
+
+        lax.fori_loop(0, alone, body, 0)
 
     @pl.when(g < last)
     def _():
@@ -533,11 +642,20 @@
     @pl.when((g > 0) & (g < last))
     def _():
         each(lambda s: send_forward(s, 0).wait_send())
-        each(lambda s: send_backward(s).wait_send())
+        all_but_lone(lambda s: send_backward(s).wait_send())
 
     @pl.when(g == last)
     def _():
-        each(lambda s: send_window(s).wait_send())
+        all_but_lone(lambda s: send_window(s).wait_send())
+
+    @pl.when(g > 0)
+    def _():
+        send_own_far().wait_send()
+
+    for m in range(2, sections):
+        @pl.when((g > 0) & (g < m))
+        def _():
+            send_far_on(m).wait_send()
 
     @pl.when(t < end)
     def _():
@@ -610,19 +728,21 @@
             pltpu.VMEM((extent, extent), f32),
             pltpu.VMEM((slots, extent, extent), bf16),
             waves, rims, rims,
-            waves, waves, waves, waves, waves,
+            waves, waves,
+            pltpu.VMEM((slots + sections - 1, 2, extent, extent), f32),
+            waves, waves,
             pltpu.VMEM((4, extent, 3 * extent), bf16),
             pltpu.VMEM((4, 3 * extent, extent), bf16),
             pltpu.VMEM((3, extent, extent), f32),
             pltpu.VMEM((2, 3 * extent, extent), bf16),
             pltpu.VMEM((2, extent, 3 * extent), bf16),
             pltpu.VMEM((2, extent, extent), f32),
-            pltpu.VMEM((2, extent, extent), f32),
             dma((3,)),
             dma((slots,)),
             dma((2, slots)),
             dma((slots, 2)), dma((slots, 2)),
             dma((slots,)), dma((slots,)),
+            dma((sections,)), dma((sections,)),
             dma((2, slots)), dma((2, slots)),
             dma((2, slots)), dma((2, slots)),
             pltpu.SemaphoreType.REGULAR,

time: 164 us -> 158 us (0.963)
  Pallas kernels: 153 us -> 147 us
    pallas_call x1, Pallas kernels: 138 us -> 132 us  [on_device(): pl.pallas_call(functools.partial(pipeline_kernel, sections, tiles), out_s...]
where the time goes in v3:
time: 158 us; the launch traced here: 157 us
  Pallas kernels  147 us (93%)
  starting transfers between devices  6.45 us (4%)
    pallas_call x1, Pallas kernels, on_device(): pl.pallas_call(functools.partial(pipeline_kernel, sections, tiles), out_s...  132 us
    pallas_call x1, Pallas kernels, on_device(): pl.pallas_call(gather_kernel, out_shape=(sds((2, rows, cols), f32), wave)...  8.79 us
    pallas_call x1, Pallas kernels, on_device(): pl.pallas_call(extract_kernel, out_shape=(wave, rim, rim), in_specs=[smem...  6.6 us
    ppermute x2, starting transfers between devices, shift(): return lax.ppermute(value, axis, pairs)  6.45 us
  transfers between devices with their start and end apart: 2, of which 0 were waited for; matrix products, arithmetic and copies ran while one was open for 0% of the time, Pallas kernels for 0%

profile of v3, /device:TPU:3, one launch (start us, length us, event | category | flops | bytes accessed | tf_op | source)
XLA Modules:
  0.0 157.4 jit_solution(17087095896704354319)
XLA Ops:
  0.6 0.7 copy.19
  1.4 0.8 pad_add_fusion.own_pos
  2.1 0.0 copy-start
  2.1 2.6 %collective-permute-start.1 = (s32[2,7]{1,0:T(2,128)S(1)}, s32[2,7]{1,0:T(2,128)S(1)}, u32[]{:S(2)}, u32[]{:S(2)}) collective-permute-start(s32[2,7]{1,0:T(2,128)S(1)} %pad_add_fusion.own_pos), channel_id=1, source_target_pairs={{1,0},{2,1},{3,2},{4,3},{5,4},{6,5},{7,6},{9,8},{10,9},{11,10},{12... | collective-permute-start | bytes 176 | tf_op jit(solution)/shard_map/ppermute | solution.py:36
  4.7 3.9 %collective-permute-start = (s32[2,7]{1,0:T(2,128)S(1)}, s32[2,7]{1,0:T(2,128)S(1)}, u32[]{:S(2)}, u32[]{:S(2)}) collective-permute-start(s32[2,7]{1,0:T(2,128)S(1)} %pad_add_fusion.own_pos), channel_id=1, source_target_pairs={{0,1},{1,2},{2,3},{3,4},{4,5},{5,6},{6,7},{8,9},{9,10},{10,11},{11... | collective-permute-start | bytes 176 | tf_op jit(solution)/shard_map/ppermute | solution.py:36
  9.2 0.0 collective-permute-done.1.right_pos
  9.2 0.0 copy-start.1
  9.3 0.0 collective-permute-done.left_pos
  9.3 0.0 copy-start.2
  9.3 0.0 copy-done
  9.3 0.5 copy-done.1
  9.8 0.0 copy-done.2
  9.9 6.6 %shard_map.176 = (f32[6,2,256,256]{3,2,1,0:T(8,128)}, f32[6,2,256,128]{3,2,1,0:T(8,128)}, f32[6,2,256,128]{3,2,1,0:T(8,128)}) custom-call(s32[2,7]{1,0:T(2,128)} %copy-done.2, s32[2,7]{1,0:T(2,128)} %copy-done.1, s32[2,7]{1,0:T(2,128)} %copy-done, f32[2,4096,256]{2,1,0:T(8,128)} %bitcast.8), custom_call_target="tpu_custom_call" | custom-call | tf_op jit(solution)/shard_map/pallas_call | solution.py:707
  16.5 132.1 %shard_map.177 = (f32[6,2,256,256]{3,2,1,0:T(8,128)}, f32[6,2,256,256]{3,2,1,0:T(8,128)}, f32[6,2,256,128]{3,2,1,0:T(8,128)}, f32[6,2,256,128]{3,2,1,0:T(8,128)}) custom-call(s32[1]{0:T(128)S(6)} %copy.20.counts, f32[6,2,256,256]{3,2,1,0:T(8,128)} %get-tuple-element.11.own, f32[6,2,256,128]{3,2,1,0:T(8,128)} %get-tuple-element.12.to_left, ...), custom_call_target="tpu_custom_call" | custom-call | tf_op jit(solution)/shard_map/pallas_call | solution.py:721
  148.6 8.8 %shard_map.178 = (f32[2,4096,256]{2,1,0:T(8,128)}, f32[6,2,256,256]{3,2,1,0:T(8,128)}) custom-call(s32[2,7]{1,0:T(2,128)} %copy-done.2, s32[2,7]{1,0:T(2,128)} %copy-done.1, s32[2,7]{1,0:T(2,128)} %copy-done, f32[6,2,256,256]{3,2,1,0:T(8,128)} %get-tuple-element.14.contrib, f32[6,2,256,128]{3,2,1,0:T(8,128)} %get-tuple-element.15.from_left, ...), custom_call_target="tpu_custom_call" | custom-call | tf_op jit(solution)/shard_map/pallas_call | solution.py:752
Async XLA Ops:
  2.1 7.2 %copy-start = (s32[2,7]{1,0:T(2,128)}, s32[2,7]{1,0:T(2,128)S(1)}, u32[]{:S(2)}) copy-start(s32[2,7]{1,0:T(2,128)S(1)} %pad_add_fusion.own_pos) | copy-start | bytes 172
  2.1 7.1 %collective-permute-start.1 = (s32[2,7]{1,0:T(2,128)S(1)}, s32[2,7]{1,0:T(2,128)S(1)}, u32[]{:S(2)}, u32[]{:S(2)}) collective-permute-start(s32[2,7]{1,0:T(2,128)S(1)} %pad_add_fusion.own_pos), channel_id=1, source_target_pairs={{1,0},{2,1},{3,2},{4,3},{5,4},{6,5},{7,6},{9,8},{10,9},{11,10},{12... | collective-permute-start | bytes 176 | tf_op jit(solution)/shard_map/ppermute | solution.py:36
  4.7 4.6 %collective-permute-start = (s32[2,7]{1,0:T(2,128)S(1)}, s32[2,7]{1,0:T(2,128)S(1)}, u32[]{:S(2)}, u32[]{:S(2)}) collective-permute-start(s32[2,7]{1,0:T(2,128)S(1)} %pad_add_fusion.own_pos), channel_id=1, source_target_pairs={{0,1},{1,2},{2,3},{3,4},{4,5},{5,6},{6,7},{8,9},{9,10},{10,11},{11... | collective-permute-start | bytes 176 | tf_op jit(solution)/shard_map/ppermute | solution.py:36
  9.2 0.6 copy-start.1
  9.3 0.6 copy-start.2

commit v4 on v3

--- a/solution.py
+++ b/solution.py
@@ -313,18 +313,25 @@
             send_sem=send_got.at[side, s], recv_sem=recv_got.at[side, s],
             device_id={"tile": t + (-1, 1)[side]}, device_id_type=MESH)
 
-    def rims_start(i):
+    yielding = (t % 2 == 0) & (t > 0)
+
+    def rims_start(side, s, ok):
+        @pl.when(ok)
+        def _():
+            rim_copy(side, s).start()
+
+    def rims_one(i):
         s = turn_of(i)
-
-        @pl.when(t > 0)
-        def _():
-            rim_copy(0, s).start()
-
-        @pl.when(t < end)
-        def _():
-            rim_copy(1, s).start()
-
-    each(rims_start)
+        rims_start(0, s, (t > 0) & jnp.logical_not(yielding))
+        rims_start(1, s, t < end)
+
+    each(rims_one)
+
+    @pl.when(yielding)
+    def _():
+        rim_copy(0, turn_of(0)).wait_recv()
+
+    each(lambda i: rims_start(0, turn_of(i), yielding))
 
     @pl.when(t == 0)
     def _():
@@ -454,7 +461,7 @@
     def compose(s):
         own_part(s).wait()
 
-        @pl.when(t < end)
+        @pl.when((t < end) & jnp.logical_not(yielding & (s == turn_of(0))))
         def _():
             rim_copy(0, s).wait_recv()
 

time: 158 us -> 155 us (0.981)
  Pallas kernels: 147 us -> 145 us
    pallas_call x1, Pallas kernels: 132 us -> 129 us  [on_device(): pl.pallas_call(functools.partial(pipeline_kernel, sections, tiles), out_s...]
where the time goes in v4:
time: 155 us
  Pallas kernels  145 us (94%)
  starting transfers between devices  6.45 us (4%)
    pallas_call x1, Pallas kernels, on_device(): pl.pallas_call(functools.partial(pipeline_kernel, sections, tiles), out_s...  129 us
    pallas_call x1, Pallas kernels, on_device(): pl.pallas_call(gather_kernel, out_shape=(sds((2, rows, cols), f32), wave)...  8.79 us
    pallas_call x1, Pallas kernels, on_device(): pl.pallas_call(extract_kernel, out_shape=(wave, rim, rim), in_specs=[smem...  6.6 us
    ppermute x2, starting transfers between devices, shift(): return lax.ppermute(value, axis, pairs)  6.45 us
  transfers between devices with their start and end apart: 2, of which 0 were waited for; matrix products, arithmetic and copies ran while one was open for 0% of the time, Pallas kernels for 0%

profile of v4, /device:TPU:3, one launch (start us, length us, event | category | flops | bytes accessed | tf_op | source)
XLA Modules:
  0.0 154.5 jit_solution(17027249277699880197)
XLA Ops:
  0.6 0.7 copy.19
  1.4 0.8 pad_add_fusion.own_pos
  2.1 0.0 copy-start
  2.1 2.6 %collective-permute-start.1 = (s32[2,7]{1,0:T(2,128)S(1)}, s32[2,7]{1,0:T(2,128)S(1)}, u32[]{:S(2)}, u32[]{:S(2)}) collective-permute-start(s32[2,7]{1,0:T(2,128)S(1)} %pad_add_fusion.own_pos), channel_id=1, source_target_pairs={{1,0},{2,1},{3,2},{4,3},{5,4},{6,5},{7,6},{9,8},{10,9},{11,10},{12... | collective-permute-start | bytes 176 | tf_op jit(solution)/shard_map/ppermute | solution.py:36
  4.7 3.9 %collective-permute-start = (s32[2,7]{1,0:T(2,128)S(1)}, s32[2,7]{1,0:T(2,128)S(1)}, u32[]{:S(2)}, u32[]{:S(2)}) collective-permute-start(s32[2,7]{1,0:T(2,128)S(1)} %pad_add_fusion.own_pos), channel_id=1, source_target_pairs={{0,1},{1,2},{2,3},{3,4},{4,5},{5,6},{6,7},{8,9},{9,10},{10,11},{11... | collective-permute-start | bytes 176 | tf_op jit(solution)/shard_map/ppermute | solution.py:36
  9.2 0.0 collective-permute-done.1.right_pos
  9.2 0.0 copy-start.1
  9.3 0.0 collective-permute-done.left_pos
  9.3 0.0 copy-start.2
  9.3 0.0 copy-done
  9.3 0.5 copy-done.1
  9.8 0.0 copy-done.2
  9.9 6.6 %shard_map.176 = (f32[6,2,256,256]{3,2,1,0:T(8,128)}, f32[6,2,256,128]{3,2,1,0:T(8,128)}, f32[6,2,256,128]{3,2,1,0:T(8,128)}) custom-call(s32[2,7]{1,0:T(2,128)} %copy-done.2, s32[2,7]{1,0:T(2,128)} %copy-done.1, s32[2,7]{1,0:T(2,128)} %copy-done, f32[2,4096,256]{2,1,0:T(8,128)} %bitcast.8), custom_call_target="tpu_custom_call" | custom-call | tf_op jit(solution)/shard_map/pallas_call | solution.py:714
  16.5 129.2 %shard_map.177 = (f32[6,2,256,256]{3,2,1,0:T(8,128)}, f32[6,2,256,256]{3,2,1,0:T(8,128)}, f32[6,2,256,128]{3,2,1,0:T(8,128)}, f32[6,2,256,128]{3,2,1,0:T(8,128)}) custom-call(s32[1]{0:T(128)S(6)} %copy.20.counts, f32[6,2,256,256]{3,2,1,0:T(8,128)} %get-tuple-element.11.own, f32[6,2,256,128]{3,2,1,0:T(8,128)} %get-tuple-element.12.to_left, ...), custom_call_target="tpu_custom_call" | custom-call | tf_op jit(solution)/shard_map/pallas_call | solution.py:728
  145.7 8.8 %shard_map.178 = (f32[2,4096,256]{2,1,0:T(8,128)}, f32[6,2,256,256]{3,2,1,0:T(8,128)}) custom-call(s32[2,7]{1,0:T(2,128)} %copy-done.2, s32[2,7]{1,0:T(2,128)} %copy-done.1, s32[2,7]{1,0:T(2,128)} %copy-done, f32[6,2,256,256]{3,2,1,0:T(8,128)} %get-tuple-element.14.contrib, f32[6,2,256,128]{3,2,1,0:T(8,128)} %get-tuple-element.15.from_left, ...), custom_call_target="tpu_custom_call" | custom-call | tf_op jit(solution)/shard_map/pallas_call | solution.py:759
Async XLA Ops:
  2.1 7.2 %copy-start = (s32[2,7]{1,0:T(2,128)}, s32[2,7]{1,0:T(2,128)S(1)}, u32[]{:S(2)}) copy-start(s32[2,7]{1,0:T(2,128)S(1)} %pad_add_fusion.own_pos) | copy-start | bytes 172
  2.1 7.1 %collective-permute-start.1 = (s32[2,7]{1,0:T(2,128)S(1)}, s32[2,7]{1,0:T(2,128)S(1)}, u32[]{:S(2)}, u32[]{:S(2)}) collective-permute-start(s32[2,7]{1,0:T(2,128)S(1)} %pad_add_fusion.own_pos), channel_id=1, source_target_pairs={{1,0},{2,1},{3,2},{4,3},{5,4},{6,5},{7,6},{9,8},{10,9},{11,10},{12... | collective-permute-start | bytes 176 | tf_op jit(solution)/shard_map/ppermute | solution.py:36
  4.7 4.6 %collective-permute-start = (s32[2,7]{1,0:T(2,128)S(1)}, s32[2,7]{1,0:T(2,128)S(1)}, u32[]{:S(2)}, u32[]{:S(2)}) collective-permute-start(s32[2,7]{1,0:T(2,128)S(1)} %pad_add_fusion.own_pos), channel_id=1, source_target_pairs={{0,1},{1,2},{2,3},{3,4},{4,5},{5,6},{6,7},{8,9},{9,10},{10,11},{11... | collective-permute-start | bytes 176 | tf_op jit(solution)/shard_map/ppermute | solution.py:36
  9.2 0.6 copy-start.1
  9.3 0.6 copy-start.2

commit v5 on v4

--- a/solution.py
+++ b/solution.py
@@ -28,12 +28,6 @@
 
 def smem():
     return pl.BlockSpec(memory_space=pltpu.SMEM)
-
-
-def shift(value, axis, by):
-    count = lax.axis_size(axis)
-    pairs = [(i, i + by) for i in range(count) if 0 <= i + by < count]
-    return lax.ppermute(value, axis, pairs)
 
 
 def make_tables(extent):
@@ -58,6 +52,57 @@
 def aligned(row, limit):
     base = jnp.minimum(row // PAD * PAD, limit)
     return pl.multiple_of(base, PAD), row - base
+
+
+def exchange_kernel(tiles, places, widths, left, right, own, box_places, box_widths, send, recv):
+    t = lax.axis_index("tile")
+    slots = places.shape[1]
+    barrier = pltpu.get_barrier_semaphore()
+    inside = (t > 0, t < tiles - 1)
+    for side in range(2):
+        @pl.when(inside[side])
+        def _():
+            pl.semaphore_signal(
+                barrier, inc=1, device_id={"tile": t + (-1, 1)[side]}, device_id_type=MESH)
+
+    def copies(side):
+        return [
+            pltpu.make_async_remote_copy(
+                src_ref=src, dst_ref=dst.at[side], send_sem=send.at[i, side],
+                recv_sem=recv.at[i, side], device_id={"tile": t + (-1, 1)[side]},
+                device_id_type=MESH)
+            for i, (src, dst) in enumerate(((places, box_places), (widths, box_widths)))
+        ]
+
+    pl.semaphore_wait(barrier, inside[0].astype(jnp.int32) + inside[1].astype(jnp.int32))
+    for side in range(2):
+        @pl.when(inside[side])
+        def _():
+            for copy in copies(side):
+                copy.start()
+
+    for k in range(2):
+        for s in range(slots):
+            own[k, s] = places[k, s]
+        own[k, slots] = widths[0, k]
+
+    for side, out in enumerate((left, right)):
+        @pl.when(inside[side])
+        def _():
+            for copy in copies(1 - side):
+                copy.wait_recv()
+            for k in range(2):
+                for s in range(slots):
+                    out[k, s] = box_places[1 - side, k, s]
+                out[k, slots] = box_widths[1 - side, 0, k]
+            for copy in copies(side):
+                copy.wait_send()
+
+        @pl.when(jnp.logical_not(inside[side]))
+        def _():
+            for k in range(2):
+                for s in range(slots + 1):
+                    out[k, s] = 0
 
 
 def extract_kernel(left_pos, right_pos, own_pos, trans, own, to_left, to_right,
@@ -700,9 +745,6 @@
     sections = lax.axis_size("cuts")
     tiles = lax.axis_size("tile")
     assert extent == cols and extent >= 2 * RIM and tiles % 2 == 0 and sections >= 2
-    own_pos = jnp.concatenate([jnp.swapaxes(positions[0], 0, 1), widths.reshape(2, 1)], 1)
-    right_pos = shift(own_pos, "tile", -1)
-    left_pos = shift(own_pos, "tile", 1)
     sds = jax.ShapeDtypeStruct
     wave = sds((slots, 2, extent, extent), f32)
     rim = sds((slots, 2, extent, RIM), f32)
@@ -711,6 +753,19 @@
     hbm = pl.BlockSpec(memory_space=pl.ANY)
     dma = pltpu.SemaphoreType.DMA
     tall = extent + PAD
+    marks = sds((2, slots + 1), jnp.int32)
+    left_pos, right_pos, own_pos = pl.pallas_call(
+        functools.partial(exchange_kernel, tiles),
+        out_shape=(marks,) * 3,
+        in_specs=[smem()] * 2,
+        out_specs=(smem(),) * 3,
+        scratch_shapes=[
+            pltpu.SMEM((2, 2, slots), jnp.int32),
+            pltpu.SMEM((2, 1, 2), jnp.int32),
+            dma((2, 2)), dma((2, 2)),
+        ],
+        compiler_params=params(EXTRACT_VMEM, collective_id=1, has_side_effects=True),
+    )(jnp.swapaxes(positions[0], 0, 1), widths)
     own, to_left, to_right = pl.pallas_call(
         extract_kernel,
         out_shape=(wave, rim, rim),

time: 155 us -> 150 us (0.968)
  starting transfers between devices: 6.45 us -> 0 us
  Pallas kernels: 145 us -> 149 us
    ppermute x2 -> x0, starting transfers between devices: 6.45 us -> none  [shift(): return lax.ppermute(value, axis, pairs)]
    pallas_call x0 -> x1, Pallas kernels: none -> 5.34 us  [on_device(): pl.pallas_call(functools.partial(exchange_kernel, tiles), out_shape=(mark...]
  transfers between devices with their start and end apart: 2 -> 0, of which waited for: 0 -> 0; matrix products, arithmetic and copies ran while one was open for 0% -> 0% of each run, Pallas kernels for 0% -> 0%
where the time goes in v5:
time: 150 us
  Pallas kernels  149 us (99%)
    pallas_call x1, Pallas kernels, on_device(): pl.pallas_call(functools.partial(pipeline_kernel, sections, tiles), out_s...  128 us
    pallas_call x1, Pallas kernels, on_device(): pl.pallas_call(gather_kernel, out_shape=(sds((2, rows, cols), f32), wave)...  8.79 us
    pallas_call x1, Pallas kernels, on_device(): pl.pallas_call(extract_kernel, out_shape=(wave, rim, rim), in_specs=[smem...  6.6 us
    pallas_call x1, Pallas kernels, on_device(): pl.pallas_call(functools.partial(exchange_kernel, tiles), out_shape=(mark...  5.34 us

profile of v5, /device:TPU:3, one launch (start us, length us, event | category | flops | bytes accessed | tf_op | source)
XLA Modules:
  0.0 150.0 jit_solution(13535782219855448816)
XLA Ops:
  1.3 5.3 %shard_map.176 = (s32[2,7]{1,0:T(2,128)}, s32[2,7]{1,0:T(2,128)}, s32[2,7]{1,0:T(2,128)}) custom-call(s32[2,6]{1,0:T(2,128)} %bitcast.11, s32[1,2]{1,0:T(1,128)} %widths.1), custom_call_target="tpu_custom_call" | custom-call | tf_op jit(solution)/shard_map/pallas_call | solution.py:757
  6.6 6.6 %shard_map.177 = (f32[6,2,256,256]{3,2,1,0:T(8,128)}, f32[6,2,256,128]{3,2,1,0:T(8,128)}, f32[6,2,256,128]{3,2,1,0:T(8,128)}) custom-call(s32[2,7]{1,0:T(2,128)} %get-tuple-element.14.left_pos, s32[2,7]{1,0:T(2,128)} %get-tuple-element.15.right_pos, s32[2,7]{1,0:T(2,128)} %get-tuple-element.16.own_pos, f32[2,4096,256]{2,1,0:T(8,128)} %bitcast.7), custom_call_target="tpu_custom_call" | custom-call | tf_op jit(solution)/shard_map/pallas_call | solution.py:769
  13.2 128.0 %shard_map.178 = (f32[6,2,256,256]{3,2,1,0:T(8,128)}, f32[6,2,256,256]{3,2,1,0:T(8,128)}, f32[6,2,256,128]{3,2,1,0:T(8,128)}, f32[6,2,256,128]{3,2,1,0:T(8,128)}) custom-call(s32[1]{0:T(128)S(6)} %copy.19.counts, f32[6,2,256,256]{3,2,1,0:T(8,128)} %get-tuple-element.17.own, f32[6,2,256,128]{3,2,1,0:T(8,128)} %get-tuple-element.18.to_left, ...), custom_call_target="tpu_custom_call" | custom-call | tf_op jit(solution)/shard_map/pallas_call | solution.py:783
  141.2 8.8 %shard_map.179 = (f32[2,4096,256]{2,1,0:T(8,128)}, f32[6,2,256,256]{3,2,1,0:T(8,128)}) custom-call(s32[2,7]{1,0:T(2,128)} %get-tuple-element.14.left_pos, s32[2,7]{1,0:T(2,128)} %get-tuple-element.15.right_pos, s32[2,7]{1,0:T(2,128)} %get-tuple-element.16.own_pos, f32[6,2,256,256]{3,2,1,0:T(8,128)} %get-tuple-element.20.contrib, ...), custom_call_target="tpu_custom_call" | custom-call | tf_op jit(solution)/shard_map/pallas_call | solution.py:814

commit v6 on v5

--- a/solution.py
+++ b/solution.py
@@ -248,7 +248,7 @@
     plan = [(0, OFFER, g)] * (0 < g < last)
     if g >= mid:
         return plan + relays + [(s, WHOLE, g) for s in range(slots)]
-    lag = 2 * (mid - g)
+    lag = 2 * (mid - g) + (g == 0)
     done = 0
     for k in range(slots):
         plan += [(k, ENTER, g)]

time: 150 us -> 149 us (level)
  no operation moved by 1% of the time
where the time goes in v6:
time: 149 us
  Pallas kernels  148 us (99%)
    pallas_call x1, Pallas kernels, on_device(): pl.pallas_call(functools.partial(pipeline_kernel, sections, tiles), out_s...  127 us
    pallas_call x1, Pallas kernels, on_device(): pl.pallas_call(gather_kernel, out_shape=(sds((2, rows, cols), f32), wave)...  8.79 us
    pallas_call x1, Pallas kernels, on_device(): pl.pallas_call(extract_kernel, out_shape=(wave, rim, rim), in_specs=[smem...  6.6 us
    pallas_call x1, Pallas kernels, on_device(): pl.pallas_call(functools.partial(exchange_kernel, tiles), out_shape=(mark...  5.34 us

profile of v6, /device:TPU:3, one launch (start us, length us, event | category | flops | bytes accessed | tf_op | source)
XLA Modules:
  0.0 149.0 jit_solution(3822970482003436507)
XLA Ops:
  1.3 5.3 %shard_map.176 = (s32[2,7]{1,0:T(2,128)}, s32[2,7]{1,0:T(2,128)}, s32[2,7]{1,0:T(2,128)}) custom-call(s32[2,6]{1,0:T(2,128)} %bitcast.11, s32[1,2]{1,0:T(1,128)} %widths.1), custom_call_target="tpu_custom_call" | custom-call | tf_op jit(solution)/shard_map/pallas_call | solution.py:757
  6.6 6.6 %shard_map.177 = (f32[6,2,256,256]{3,2,1,0:T(8,128)}, f32[6,2,256,128]{3,2,1,0:T(8,128)}, f32[6,2,256,128]{3,2,1,0:T(8,128)}) custom-call(s32[2,7]{1,0:T(2,128)} %get-tuple-element.14.left_pos, s32[2,7]{1,0:T(2,128)} %get-tuple-element.15.right_pos, s32[2,7]{1,0:T(2,128)} %get-tuple-element.16.own_pos, f32[2,4096,256]{2,1,0:T(8,128)} %bitcast.7), custom_call_target="tpu_custom_call" | custom-call | tf_op jit(solution)/shard_map/pallas_call | solution.py:769
  13.2 127.0 %shard_map.178 = (f32[6,2,256,256]{3,2,1,0:T(8,128)}, f32[6,2,256,256]{3,2,1,0:T(8,128)}, f32[6,2,256,128]{3,2,1,0:T(8,128)}, f32[6,2,256,128]{3,2,1,0:T(8,128)}) custom-call(s32[1]{0:T(128)S(6)} %copy.19.counts, f32[6,2,256,256]{3,2,1,0:T(8,128)} %get-tuple-element.17.own, f32[6,2,256,128]{3,2,1,0:T(8,128)} %get-tuple-element.18.to_left, ...), custom_call_target="tpu_custom_call" | custom-call | tf_op jit(solution)/shard_map/pallas_call | solution.py:783
  140.2 8.8 %shard_map.179 = (f32[2,4096,256]{2,1,0:T(8,128)}, f32[6,2,256,256]{3,2,1,0:T(8,128)}) custom-call(s32[2,7]{1,0:T(2,128)} %get-tuple-element.14.left_pos, s32[2,7]{1,0:T(2,128)} %get-tuple-element.15.right_pos, s32[2,7]{1,0:T(2,128)} %get-tuple-element.16.own_pos, f32[6,2,256,256]{3,2,1,0:T(8,128)} %get-tuple-element.20.contrib, ...), custom_call_target="tpu_custom_call" | custom-call | tf_op jit(solution)/shard_map/pallas_call | solution.py:814
